TPU v7x, 32 devices: a whole 2x2x4 slice. The times are simulated.
32 devices in a mesh: row: 8 (over y, x, core), col: 4 (over z).
Axes of the slice: x: 2, y: 2, z: 4, core: 2. Of those that a mesh axis runs over, the one named last changes fastest.
Arguments:
- velocity: float32 [3, 2, 128, 256, 256], P(None, None, 'row', 'col'), may hold values from -7.5 to 7.5
- accumulator: float32 [3, 2, 128, 256, 256], P(None, None, 'row', 'col'), may hold values from -6 to 6
- remesh_flag: int32 [128], P('row'), may hold values 0 or 1
- remesh_shift: int32 [128], P('row'), may hold values from -128 to 127
- viscosity: float32 [1], replicated, may hold values from 0.0003 to 0.0015
- shear: float32 [1], replicated, may hold values from 8 to 20
- clock: float32 [1], replicated, may hold values from 0 to 0.05
- step: float32 [1], replicated, may hold values from 0.004 to 0.01
Outputs:
- new_velocity: float32 [3, 2, 128, 256, 256], P(None, None, 'row', 'col')
- new_accumulator: float32 [3, 2, 128, 256, 256], P(None, None, 'row', 'col')
- spectra: float32 [2, 128], P(None, 'row')
All inputs are finite; a program needn't handle non-finite values. No bound on the sum of `remesh_flag` on one device may be relied on, other than what follows from the above.
Results may differ from a plain program's by a relative error of at most 0.0001.
Values sent between devices are 32-bit elements; how exact they have to be, the bound alone decides.
No kernel may reach another device: no remote copies, remote signals or barrier semaphores. Data moves between devices by JAX's collectives and lax.ppermute only.
A program may use at most 192 MiB of HBM per device.

v0:
```python
import functools
import math

import jax
import jax.numpy as jnp
import numpy as np
from jax import lax
from jax.experimental import pallas as pl
from jax.experimental.pallas import tpu as pltpu
from jax.sharding import PartitionSpec as P


F32 = jnp.float32
BF16 = jnp.bfloat16
VMEM_LIMIT = 56 * 1024 * 1024


def signed_index(positions, period):
    return jnp.where(2 * positions < period, positions, positions - period)


def roll_rows(field, amounts):

    def shift_row(row_data, amount_one):
        return jnp.roll(row_data, -amount_one, axis=-1)

    return jax.vmap(shift_row, in_axes=(2, 0), out_axes=2)(field, amounts)


def dft_tables(period):
    positions = jnp.arange(period, dtype=jnp.int32)
    product = positions[:, None] * positions[None, :] % period
    angles = product.astype(jnp.float32) * (2.0 * math.pi / period)
    factor = 1.0 / math.sqrt(period)
    return (jnp.cos(angles) * factor, jnp.sin(angles) * factor)


def product_high(formula, first_arg, second_arg):
    return jnp.einsum(formula, first_arg, second_arg, precision=lax.Precision.HIGHEST)


def rotate(left_side, right_side, output, real_part, imag_part, cosine_table, sine_table, backward):
    stacked = jnp.stack([real_part, imag_part])
    if backward:
        block_table = jnp.stack(
            [jnp.stack([cosine_table, sine_table]), jnp.stack([-sine_table, cosine_table])]
        )
    else:
        block_table = jnp.stack(
            [jnp.stack([cosine_table, -sine_table]), jnp.stack([sine_table, cosine_table])]
        )
    result = product_high(
        "s" + left_side + ",st" + right_side + "->t" + output, stacked, block_table
    )
    return (result[0], result[1])


def project(real_part, imag_part, wave_vector, inverse_square):
    along_real = (
        wave_vector[0] * real_part[0]
        + wave_vector[1] * real_part[1]
        + wave_vector[2] * real_part[2]
    ) * inverse_square
    along_imag = (
        wave_vector[0] * imag_part[0]
        + wave_vector[1] * imag_part[1]
        + wave_vector[2] * imag_part[2]
    ) * inverse_square
    return (
        jnp.stack([real_part[number] - wave_vector[number] * along_real for number in range(3)]),
        jnp.stack([imag_part[number] - wave_vector[number] * along_imag for number in range(3)]),
    )


def cross_product(first_one, second_one):
    return jnp.stack(
        [
            first_one[1] * second_one[2] - first_one[2] * second_one[1],
            first_one[2] * second_one[0] - first_one[0] * second_one[2],
            first_one[0] * second_one[1] - first_one[1] * second_one[0],
        ]
    )


def to_physical(real_part, imag_part, tables_all):
    (cos_y, sin_y), (cos_x, sin_x), (cos_z, sin_z) = tables_all
    row_count = lax.axis_size("row")
    col_count = lax.axis_size("col")
    fields, width_x, width_z, full_y = real_part.shape
    block_y = full_y // row_count
    half_x = width_x * row_count
    full_x = cos_x.shape[0]
    block_x = full_x // col_count
    full_z = width_z * col_count
    shape_y = (full_y, row_count, block_y)
    first_real, first_imag = rotate(
        "fabc",
        "cpq",
        "fpabq",
        real_part,
        imag_part,
        cos_y.reshape(shape_y),
        sin_y.reshape(shape_y),
        True,
    )
    flat_shape = (fields, row_count, width_x, width_z * block_y)
    second_real, second_imag = (
        lax.all_to_all(
            first_real.reshape(flat_shape), "row", split_axis=1, concat_axis=2, tiled=True
        ),
        lax.all_to_all(
            first_imag.reshape(flat_shape), "row", split_axis=1, concat_axis=2, tiled=True
        ),
    )
    deep_shape = (fields, half_x, width_z, block_y)
    weights = jnp.where(jnp.arange(half_x) == 0, 1.0, 2.0).astype(jnp.float32)[:, None]
    shape_x = (half_x, col_count, block_x)
    cos_half = (weights * cos_x[:half_x]).reshape(shape_x)
    sin_half = (weights * sin_x[:half_x]).reshape(shape_x)
    third_real, third_imag = rotate(
        "fkzy",
        "kpq",
        "fpzyq",
        second_real.reshape(deep_shape),
        second_imag.reshape(deep_shape),
        cos_half,
        sin_half,
        True,
    )
    flat_shape = (fields, col_count, 1, width_z * block_y * block_x)
    fourth_real, fourth_imag = (
        lax.all_to_all(
            third_real.reshape(flat_shape), "col", split_axis=1, concat_axis=2, tiled=True
        ),
        lax.all_to_all(
            third_imag.reshape(flat_shape), "col", split_axis=1, concat_axis=2, tiled=True
        ),
    )
    deep_shape = (fields, col_count, width_z, block_y, block_x)
    shape_z = (col_count, width_z, full_z)
    stacked = jnp.stack([fourth_real.reshape(deep_shape), fourth_imag.reshape(deep_shape)])
    z_table = jnp.stack([cos_z.reshape(shape_z), -sin_z.reshape(shape_z)])
    return product_high("sfpkyq,spkn->fyqn", stacked, z_table)


def to_spectral(physical, tables_all, half_x):
    (cos_y, sin_y), (cos_x, sin_x), (cos_z, sin_z) = tables_all
    row_count = lax.axis_size("row")
    col_count = lax.axis_size("col")
    fields, block_y, block_x, full_z = physical.shape
    width_z = full_z // col_count
    width_x = half_x // row_count
    full_y = block_y * row_count
    shape_z = (full_z, col_count, width_z)
    z_table = jnp.stack([cos_z.reshape(shape_z), -sin_z.reshape(shape_z)])
    first_both = product_high("fyqn,tnpk->tfpkyq", physical, z_table)
    first_real, first_imag = (first_both[0], first_both[1])
    flat_shape = (fields, col_count, 1, width_z * block_y * block_x)
    second_real, second_imag = (
        lax.all_to_all(
            first_real.reshape(flat_shape), "col", split_axis=1, concat_axis=2, tiled=True
        ),
        lax.all_to_all(
            first_imag.reshape(flat_shape), "col", split_axis=1, concat_axis=2, tiled=True
        ),
    )
    deep_shape = (fields, col_count, width_z, block_y, block_x)
    shape_x = (col_count, block_x, row_count, width_x)
    third_real, third_imag = rotate(
        "fpkyq",
        "pqmr",
        "fmrky",
        second_real.reshape(deep_shape),
        second_imag.reshape(deep_shape),
        cos_x[:, :half_x].reshape(shape_x),
        sin_x[:, :half_x].reshape(shape_x),
        False,
    )
    flat_shape = (fields, row_count, 1, width_x * width_z * block_y)
    fourth_real, fourth_imag = (
        lax.all_to_all(
            third_real.reshape(flat_shape), "row", split_axis=1, concat_axis=2, tiled=True
        ),
        lax.all_to_all(
            third_imag.reshape(flat_shape), "row", split_axis=1, concat_axis=2, tiled=True
        ),
    )
    deep_shape = (fields, row_count, width_x, width_z, block_y)
    shape_y = (row_count, block_y, full_y)
    return rotate(
        "fparq",
        "pqn",
        "farn",
        fourth_real.reshape(deep_shape),
        fourth_imag.reshape(deep_shape),
        cos_y.reshape(shape_y),
        sin_y.reshape(shape_y),
        False,
    )


def many_physical(real_part, imag_part, tables_all):
    return jnp.concatenate(
        [
            to_physical(real_part[number : number + 1], imag_part[number : number + 1], tables_all)
            for number in range(real_part.shape[0])
        ]
    )


def many_spectral(physical, tables_all, half_x):
    result_list = [
        to_spectral(physical[number : number + 1], tables_all, half_x)
        for number in range(physical.shape[0])
    ]
    return (
        jnp.concatenate([entry[0] for entry in result_list]),
        jnp.concatenate([entry[1] for entry in result_list]),
    )


def body(velocity, accumulator, remesh_flag, remesh_shift, viscosity, shear, clock, step):
    width_x = velocity.shape[2]
    width_z = velocity.shape[3]
    full_y = velocity.shape[4]
    half_x = width_x * lax.axis_size("row")
    NX, NY, NZ = 2 * half_x, full_y, width_z * lax.axis_size("col")
    offset = remesh_flag * remesh_shift
    remeshed = roll_rows(velocity, offset)
    carried = roll_rows(accumulator, offset)
    lattice_x = lax.axis_index("row") * width_x + jnp.arange(width_x, dtype=jnp.int32)
    col_index = lax.axis_index("col") * width_z + jnp.arange(width_z, dtype=jnp.int32)
    lattice_z = signed_index(col_index, NZ)
    lattice_y = signed_index(jnp.arange(full_y, dtype=jnp.int32), NY)
    wave_x = lattice_x.astype(jnp.float32)[:, None, None]
    wave_z = lattice_z.astype(jnp.float32)[None, :, None]
    wave_y = lattice_y.astype(jnp.float32)[None, None, :] - shear[0] * clock[0] * wave_x
    wave_vector = (wave_x, wave_y, wave_z)
    square_wave = wave_x * wave_x + wave_y * wave_y + wave_z * wave_z
    inverse_square = 1.0 / jnp.maximum(square_wave, 1.0)
    dealias_mask = (
        (3 * lattice_x < NX)[:, None, None]
        & (3 * jnp.abs(lattice_z) < NZ)[None, :, None]
        & (3 * jnp.abs(lattice_y) < NY)[None, None, :]
    ).astype(jnp.float32)
    shear_rate = shear[0]
    viscous_rate = viscosity[0]
    stress_part = jnp.sum(
        remeshed[0, 0] * remeshed[1, 0] + remeshed[0, 1] * remeshed[1, 1], axis=(1, 2)
    )
    energy = jnp.sum(remeshed * remeshed, axis=(0, 1))
    dissipation_part = jnp.sum(square_wave * energy, axis=(1, 2))
    stress_total, dissipation_total = lax.psum((stress_part, dissipation_part), "col")
    solen_real, solen_imag = project(remeshed[:, 0], remeshed[:, 1], wave_vector, inverse_square)
    smooth_real = dealias_mask * solen_real
    smooth_imag = dealias_mask * solen_imag
    tables_all = (dft_tables(NY), dft_tables(NX), dft_tables(NZ))
    vort_real = -cross_product(wave_vector, smooth_imag)
    vort_imag = cross_product(wave_vector, smooth_real)
    both_real = jnp.concatenate([smooth_real, vort_real])
    both_imag = jnp.concatenate([smooth_imag, vort_imag])
    physical = many_physical(both_real, both_imag, tables_all)
    lamb_grid = cross_product(physical[:3], physical[3:])
    modes_real, modes_imag = many_spectral(lamb_grid, tables_all, half_x)
    hat_real = dealias_mask * modes_real
    hat_imag = dealias_mask * modes_imag
    proj_real, proj_imag = project(hat_real, hat_imag, wave_vector, inverse_square)
    coupling = 2.0 * shear_rate * wave_x * inverse_square

    def tendency(projected, state):
        term_list = [
            projected[number]
            + coupling * wave_vector[number] * state[1]
            - viscous_rate * square_wave * state[number]
            for number in range(3)
        ]
        term_list[0] = term_list[0] - shear_rate * state[1]
        return jnp.stack(term_list)

    tendencies = jnp.stack(
        [tendency(proj_real, remeshed[:, 0]), tendency(proj_imag, remeshed[:, 1])], axis=1
    )
    new_accumulator = -5.0 / 9.0 * carried + step[0] * tendencies
    new_velocity = remeshed + 15.0 / 16.0 * new_accumulator
    stress = stress_total / (NY * NZ)
    dissipation = 2.0 * viscous_rate * dissipation_total / (NY * NZ)
    return (new_velocity, new_accumulator, jnp.stack([stress, dissipation]))


def angle(rows, cols, n):
    product = np.outer(rows, cols) % n
    return np.cos(2 * np.pi * product / n) / math.sqrt(n), np.sin(2 * np.pi * product / n) / math.sqrt(n)


def halves(table):
    table = np.asarray(table, np.float32)
    high = table.astype(jnp.bfloat16)
    low = (table - high.astype(np.float32)).astype(jnp.bfloat16)
    return jnp.asarray(high), jnp.asarray(low)


def split(x):
    high = x.astype(BF16)
    return high, (x - high.astype(F32)).astype(BF16)


def dot(a, b, dims):
    return lax.dot_general(a, b, (dims, ((), ())), preferred_element_type=F32)


class Sizes:
    def __init__(self, rows, cols, width_x, width_z, full_y):
        self.rows, self.cols = rows, cols
        self.width_x, self.width_z = width_x, width_z
        self.half_x = width_x * rows
        self.full_x = 2 * self.half_x
        self.full_z = width_z * cols
        self.full_y = full_y
        self.block_y = full_y // (rows * cols)
        live = (self.full_x - 1) // 3 + 1
        self.live_x = -(-live // 8) * 8
        self.lanes = 2 * width_z

    def fits(self):
        return (
            self.block_y == 8
            and self.lanes == 128
            and self.full_y % 128 == 0
            and self.full_z % 128 == 0
            and self.full_x % 128 == 0
            and self.width_x % 2 == 0
            and self.rows & (self.rows - 1) == 0
            and self.cols & (self.cols - 1) == 0
        )


def constant_tables(s):
    c, n = angle(np.arange(s.full_y), np.arange(s.full_y), s.full_y)
    y_back = np.concatenate([c, -n], axis=1)
    y_fore = np.concatenate([c, n], axis=1)
    live = np.arange(s.live_x)
    weight = np.where(live == 0, 1.0, 2.0) * (3 * live < s.full_x)
    c, n = angle(np.arange(s.full_x), live, s.full_x)
    x_back = np.concatenate([c * weight, -n * weight], axis=1)
    x_fore = np.concatenate([c.T, -n.T], axis=0)
    c, n = angle(np.arange(s.full_z), np.arange(s.full_z), s.full_z)
    c3, n3 = c.reshape(s.cols, s.width_z, s.full_z), n.reshape(s.cols, s.width_z, s.full_z)
    z_back = np.concatenate(
        [np.concatenate([c3, n3], axis=2), np.concatenate([-n3, c3], axis=2)], axis=1
    )
    ct, nt = c3.transpose(0, 2, 1), n3.transpose(0, 2, 1)
    z_fore = np.concatenate(
        [np.concatenate([ct, -nt], axis=2), np.concatenate([nt, ct], axis=2)], axis=1
    )
    return [halves(t) for t in (y_back, y_fore, x_back, x_fore, z_back, z_fore)]


def whole(shape):
    return pl.BlockSpec(shape, lambda *_: (0,) * len(shape))


def waves(s, kx, col, shear_clock):
    plane = (s.width_z, s.full_y)
    iz = lax.broadcasted_iota(jnp.int32, plane, 0) + col * s.width_z
    iz = jnp.where(2 * iz < s.full_z, iz, iz - s.full_z)
    iy = lax.broadcasted_iota(jnp.int32, plane, 1)
    iy = jnp.where(2 * iy < s.full_y, iy, iy - s.full_y)
    k0 = kx.astype(F32)
    k1 = iy.astype(F32) - shear_clock * k0
    k2 = iz.astype(F32)
    ksq = k0 * k0 + k1 * k1 + k2 * k2
    inverse = 1.0 / jnp.maximum(ksq, 1.0)
    inside = (3 * jnp.abs(iz) < s.full_z) & (3 * jnp.abs(iy) < s.full_y) & (3 * kx < s.full_x)
    return k0, k1, k2, ksq, inverse, inside.astype(F32)


def rolled(s, ref, j, amount):
    flat = jnp.concatenate([ref[c, p, j] for c in range(3) for p in range(2)], axis=0)
    flat = pltpu.roll(flat, lax.rem(s.full_y - amount, s.full_y), 1)
    w = s.width_z
    return [[flat[(2 * c + p) * w : (2 * c + p + 1) * w] for p in range(2)] for c in range(3)]


def head_kernel(s, ints, floats, vel, yh, yl, *outs):
    fields, sums = outs[:3], outs[3]
    row, col = ints[0], ints[1]
    step = pl.program_id(0)
    right = [[], [], []]
    for j in range(2):
        local = 2 * step + j
        kx = row * s.width_x + local
        v = rolled(s, vel, j, ints[2 + local])
        k0, k1, k2, ksq, inverse, mask = waves(s, kx, col, floats[0])
        stress = v[0][0] * v[1][0] + v[0][1] * v[1][1]
        energy = sum(v[c][p] * v[c][p] for c in range(3) for p in range(2))
        fold = lambda a: jnp.sum(a.reshape(s.width_z // 8, 8, s.full_y), axis=0)
        sums[j, 0] = fold(stress)
        sums[j, 1] = fold(ksq * energy)
        along = [(k0 * v[0][p] + k1 * v[1][p] + k2 * v[2][p]) * inverse for p in range(2)]
        for c, k in enumerate((k0, k1, k2)):
            (rh, rl), (ih, il) = [split(mask * (v[c][p] - k * along[p])) for p in range(2)]
            right[c].append(jnp.concatenate([rh, ih, rl, il, rh, ih], axis=1))
            right[c].append(jnp.concatenate([ih, -rh, il, -rl, ih, -rh], axis=1))
    left = jnp.concatenate([yh[...], yh[...], yl[...]], axis=1)
    for c in range(3):
        out = dot(left, jnp.concatenate(right[c], axis=0), ((1,), (1,)))
        for r in range(s.rows):
            for q in range(s.cols):
                at = (r * s.cols + q) * 8
                for j in range(2):
                    fields[c][r, q ^ col, j] = out[at : at + 8, j * 128 : (j + 1) * 128]


def head(s, ints, floats, velocity, table):
    y2 = (s.full_y, 2 * s.full_y)
    piece = (s.rows, s.cols, s.width_x, 8, s.lanes)
    return pl.pallas_call(
        functools.partial(head_kernel, s),
        grid=(s.width_x // 2,),
        in_specs=[
            pl.BlockSpec(memory_space=pltpu.SMEM),
            pl.BlockSpec(memory_space=pltpu.SMEM),
            pl.BlockSpec((3, 2, 2, s.width_z, s.full_y), lambda i: (0, 0, i, 0, 0)),
            whole(y2),
            whole(y2),
        ],
        out_specs=[pl.BlockSpec((s.rows, s.cols, 2, 8, s.lanes), lambda i: (0, 0, i, 0, 0))] * 3
        + [pl.BlockSpec((2, 2, 8, s.full_y), lambda i: (i, 0, 0, 0))],
        out_shape=[jax.ShapeDtypeStruct(piece, F32)] * 3
        + [jax.ShapeDtypeStruct((s.width_x, 2, 8, s.full_y), F32)],
        compiler_params=pltpu.CompilerParams(vmem_limit_bytes=VMEM_LIMIT),
        name="head",
    )(ints, floats, velocity, *table)


def grid_kernel(s, ints, *refs):
    pieces, (zh, zl, xh, xl, out, mid) = refs[: s.cols], refs[s.cols :]
    col = ints[1]
    rows = s.live_x * 8
    step = rows // 4
    zt = jnp.concatenate(
        [zh[q ^ col] for q in range(s.cols)] * 2 + [zl[q ^ col] for q in range(s.cols)], axis=0
    )

    def along_z(i, carry):
        at = pl.multiple_of(i * (step // 8), step // 8)
        parts = [split(p[pl.ds(at, step // 8)].reshape(step, s.lanes)) for p in pieces]
        highs, lows = [h for h, _ in parts], [l for _, l in parts]
        left = jnp.concatenate(highs + lows + highs, axis=1)
        full = dot(left, zt, ((1,), (0,)))
        for t in range(2 * s.full_z // 128):
            mid[t, pl.ds(pl.multiple_of(i * step, step), step)] = full[:, t * 128 : (t + 1) * 128]
        return carry

    lax.fori_loop(0, 4, along_z, 0)
    xt = jnp.concatenate([xh[...], xh[...], xl[...]], axis=1)

    def along_x(y, carry):
        tiles = [mid[t, pl.ds(y, s.live_x, stride=8)] for t in range(2 * s.full_z // 128)]
        half = s.full_z // 128
        both = [jnp.concatenate(tiles[:half], axis=1), jnp.concatenate(tiles[half:], axis=1)]
        high, low = split(jnp.concatenate(both, axis=0))
        out[y] = dot(xt, jnp.concatenate([high, low, high], axis=0), ((1,), (0,)))
        return carry

    lax.fori_loop(0, 8, along_x, 0)


def to_grid(s, ints, pieces, z_table, x_table):
    rows = s.live_x * 8
    return pl.pallas_call(
        functools.partial(grid_kernel, s),
        in_specs=[pl.BlockSpec(memory_space=pltpu.SMEM)]
        + [pl.BlockSpec(memory_space=pltpu.VMEM)] * (s.cols + 4),
        out_specs=pl.BlockSpec(memory_space=pltpu.VMEM),
        out_shape=jax.ShapeDtypeStruct((8, s.full_x, s.full_z), F32),
        scratch_shapes=[pltpu.VMEM((2 * s.full_z // 128, rows, 128), F32)],
        compiler_params=pltpu.CompilerParams(vmem_limit_bytes=VMEM_LIMIT),
        name="to_grid",
    )(ints, *pieces, *z_table, *x_table)


def turn(s, rows, base, kz):
    k0 = ((lax.broadcasted_iota(jnp.int32, (rows, s.lanes), 0) + base) // 8).astype(F32)
    square = k0 * k0 + kz * kz
    scale = lax.rsqrt(jnp.maximum(square, 1.0))
    return jnp.where(square > 0, k0 * scale, 1.0), kz * scale


def back_kernel(s, which, ints, *refs):
    given, _, made = BACK[which]
    u, refs = refs[:given], refs[given:]
    saved, refs = (refs[: s.cols], refs[s.cols :]) if which == 2 else (None, refs)
    (xh, xl, zh, zl), refs = refs[:4], refs[4:]
    outs, mids = refs[: made * s.cols], refs[made * s.cols :]
    col = ints[1]
    xt = jnp.concatenate([xh[...], xh[...], xl[...]], axis=1)

    def along_x(y, carry):
        w = [ref[y] for ref in u]
        if which == 0:
            terms = [w[0] * w[0] - w[1] * w[1], w[0] * w[1]]
        elif which == 1:
            terms = [w[0] * w[1], w[1] * w[2]]
        else:
            terms = [w[0] * w[0] - w[1] * w[1]]
        for mid, term in zip(mids, terms):
            high, low = split(term)
            out = dot(xt, jnp.concatenate([high, low, high], axis=0), ((1,), (0,)))
            half = s.full_z // 128
            for t in range(2 * half):
                p, at = t // half, (t % half) * 128
                tile = out[p * s.live_x : (p + 1) * s.live_x, at : at + 128]
                mid[t, pl.ds(y, s.live_x, stride=8)] = tile
        return carry

    lax.fori_loop(0, 8, along_x, 0)
    rows = s.live_x * 8
    step = rows // 4
    zt = [jnp.concatenate([zh[q ^ col], zh[q ^ col], zl[q ^ col]], axis=0) for q in range(s.cols)]
    zt = jnp.concatenate(zt, axis=1)

    def along_z(i, carry):
        at = pl.multiple_of(i * step, step)
        done = []
        for mid in mids:
            high, low = split(
                jnp.concatenate([mid[t, pl.ds(at, step)] for t in range(2 * s.full_z // 128)], axis=1)
            )
            done.append(dot(jnp.concatenate([high, low, high], axis=1), zt, ((1,), (0,))))
        here = pl.ds(pl.multiple_of(i * (step // 8), step // 8), step // 8)
        shape = (step // 8, 8, s.lanes)
        for q in range(s.cols):
            part = [d[:, q * s.lanes : (q + 1) * s.lanes] for d in done]
            if which == 2:
                outs[q][here] = part[0].reshape(shape) - saved[q][here]
                continue
            lane = lax.broadcasted_iota(jnp.int32, (step, s.lanes), 1)
            iz = lax.rem(lane, s.width_z) + (q ^ col) * s.width_z
            kz = jnp.where(2 * iz < s.full_z, iz, iz - s.full_z).astype(F32)
            cosine, sine = turn(s, step, i * step, kz)
            if which == 0:
                first = cosine * sine * part[0] + (sine * sine - cosine * cosine) * part[1]
                second = cosine * (cosine * part[0] + 2.0 * sine * part[1])
            else:
                first = sine * part[0] - cosine * part[1]
                second = cosine * part[0] + sine * part[1]
            outs[q][here] = first.reshape(shape)
            outs[s.cols + q][here] = second.reshape(shape)
        return carry

    lax.fori_loop(0, 4, along_z, 0)


BACK = ((2, 2, 2), (3, 2, 2), (2, 1, 1))


def products(s, which, ints, fields, x_table, z_table):
    rows = s.live_x * 8
    _, number, made = BACK[which]
    piece = jax.ShapeDtypeStruct((s.live_x, 8, s.lanes), F32)
    out = pl.pallas_call(
        functools.partial(back_kernel, s, which),
        in_specs=[pl.BlockSpec(memory_space=pltpu.SMEM)]
        + [pl.BlockSpec(memory_space=pltpu.VMEM)] * (len(fields) + 4),
        out_specs=[pl.BlockSpec(memory_space=pltpu.VMEM)] * (made * s.cols),
        out_shape=[piece] * (made * s.cols),
        scratch_shapes=[pltpu.VMEM((2 * s.full_z // 128, rows, 128), F32)] * number,
        compiler_params=pltpu.CompilerParams(vmem_limit_bytes=VMEM_LIMIT),
    )(ints, *fields, *x_table, *z_table)
    return [out[i * s.cols : (i + 1) * s.cols] for i in range(made)]


def tail_kernel(s, ints, floats, vel, acc, fa, fb, fc, ff, yh, yl, new_vel, new_acc):
    row, col = ints[0], ints[1]
    local = pl.program_id(0)
    kx = row * s.width_x + local
    amount = ints[2 + local]
    right = jnp.concatenate([yh[...], yh[...], yl[...]], axis=0)
    modes = []
    for ref in (fa, fb, fc, ff):
        tiles = [ref[r, q ^ col, 0] for r in range(s.rows) for q in range(s.cols)]
        high, low = split(jnp.concatenate(tiles, axis=0).T)
        both = dot(jnp.concatenate([high, low, high], axis=1), right, ((1,), (0,)))
        w, n = s.width_z, s.full_y
        modes.append((both[:w, :n] + both[w:, n:], both[w:, :n] - both[:w, n:]))
    k0, k1, k2, ksq, inverse, mask = waves(s, kx, col, floats[0])
    flat = k0 * k0 + k2 * k2
    scale = lax.rsqrt(jnp.maximum(flat, 1.0))
    cosine, sine = jnp.where(flat > 0, k0 * scale, 1.0), k2 * scale
    kh = flat * scale
    lean = (flat - k1 * k1) * inverse
    cross = kh * k1 * inverse
    v = rolled(s, vel, 0, amount)
    old = rolled(s, acc, 0, amount)
    shear, viscosity, dt = floats[1], floats[2], floats[3]
    coupling = (2.0 * shear) * k0 * inverse
    for p in range(2):
        a, b, c, f = [m[1 - p] for m in modes]
        sign = mask if p == 0 else -mask
        qt = (kh * a + k1 * b) * sign
        qe = (lean * c + cross * f) * sign
        slope = qe * k1
        nonlinear = (qt * sine - slope * cosine, qe * kh, -(qt * cosine) - slope * sine)
        drive = coupling * v[1][p]
        for c3, k in enumerate((k0, k1, k2)):
            rate = nonlinear[c3] + k * drive - (viscosity * ksq) * v[c3][p]
            if c3 == 0:
                rate = rate - shear * v[1][p]
            fresh = (-5.0 / 9.0) * old[c3][p] + dt * rate
            new_acc[c3, p, 0] = fresh
            new_vel[c3, p, 0] = v[c3][p] + (15.0 / 16.0) * fresh


def tail(s, ints, floats, velocity, accumulator, fields, table):
    plane = pl.BlockSpec((3, 2, 1, s.width_z, s.full_y), lambda i: (0, 0, i, 0, 0))
    piece = pl.BlockSpec((s.rows, s.cols, 1, 8, s.lanes), lambda i: (0, 0, i, 0, 0))
    y2 = (s.full_y, 2 * s.full_y)
    shape = jax.ShapeDtypeStruct(velocity.shape, F32)
    return pl.pallas_call(
        functools.partial(tail_kernel, s),
        grid=(s.width_x,),
        in_specs=[pl.BlockSpec(memory_space=pltpu.SMEM)] * 2 + [plane] * 2 + [piece] * 4 + [whole(y2)] * 2,
        out_specs=[plane] * 2,
        out_shape=[shape] * 2,
        compiler_params=pltpu.CompilerParams(vmem_limit_bytes=VMEM_LIMIT),
        name="tail",
    )(ints, floats, velocity, accumulator, *fields, *table)


def col_exchange(s, pieces):
    out = [pieces[0]]
    for q in range(1, s.cols):
        out.append(lax.ppermute(pieces[q], "col", [(i, i ^ q) for i in range(s.cols)]))
    return out


def row_exchange(field):
    return lax.all_to_all(field, "row", 0, 0, tiled=True)


def forward_field(s, field):
    got = row_exchange(field)
    pieces = [
        got[:, q].reshape(s.half_x, 8, s.lanes)[: s.live_x] for q in range(s.cols)
    ]
    return col_exchange(s, pieces)


def backward_field(s, pieces):
    got = col_exchange(s, pieces)
    spare = ((0, s.half_x - s.live_x), (0, 0), (0, 0))
    both = jnp.stack(
        [jnp.pad(p, spare).reshape(s.rows, s.width_x, 8, s.lanes) for p in got], axis=1
    )
    return row_exchange(both)


def tiled_body(s, velocity, accumulator, remesh_flag, remesh_shift, viscosity, shear, clock, step):
    y_back, y_fore, x_back, x_fore, z_back, z_fore = constant_tables(s)
    place = jnp.stack([lax.axis_index("row"), lax.axis_index("col")]).astype(jnp.int32)
    ints = jnp.concatenate([place, remesh_flag * remesh_shift])
    floats = jnp.concatenate([shear * clock, shear, viscosity, step])
    v0, v1, v2, sums = head(s, ints, floats, velocity, y_back)

    def up(field):
        return to_grid(s, ints, forward_field(s, field), z_back, x_back)

    u0, u2, u1 = up(v0), up(v2), up(v1)
    a, kept = products(s, 0, ints, [u0, u2], x_fore, z_fore)
    b, c = products(s, 1, ints, [u0, u1, u2], x_fore, z_fore)
    (f,) = products(s, 2, ints, [u1, u2, *kept], x_fore, z_fore)
    a, b, c, f = [backward_field(s, q) for q in (a, b, c, f)]
    totals = lax.psum(jnp.sum(sums, axis=(2, 3)), "col") / (s.full_y * s.full_z)
    spectra = jnp.stack([totals[:, 0], 2.0 * viscosity[0] * totals[:, 1]])
    new_velocity, new_accumulator = tail(
        s, ints, floats, velocity, accumulator, (a, b, c, f), y_fore
    )
    return new_velocity, new_accumulator, spectra


def solution(mesh):
    in_specs = (
        P(None, None, "row", "col", None),
        P(None, None, "row", "col", None),
        P("row"),
        P("row"),
        P(),
        P(),
        P(),
        P(),
    )
    out_specs = (
        P(None, None, "row", "col", None),
        P(None, None, "row", "col", None),
        P(None, "row"),
    )
    rows, cols = mesh.shape["row"], mesh.shape["col"]

    def local(velocity, *rest):
        s = Sizes(rows, cols, velocity.shape[2], velocity.shape[3], velocity.shape[4])
        run = functools.partial(tiled_body, s) if s.fits() else body
        return run(velocity, *rest)

    return jax.shard_map(local, mesh=mesh, in_specs=in_specs, out_specs=out_specs, check_vma=False)
```

profile of v0, /device:TPU:0, one launch (start us, length us, event | category | flops | bytes accessed | tf_op | source)
XLA Modules:
  0.0 432.4 jit_solution(11832231127055901215)
XLA Ops:
  5.2 12.4 %head.1 = (f32[8,4,16,8,128]{4,3,2,1,0:T(8,128)}, f32[8,4,16,8,128]{4,3,2,1,0:T(8,128)}, f32[8,4,16,8,128]{4,3,2,1,0:T(8,128)}, f32[16,2,8,256]{3,2,1,0:T(8,128)}) custom-call(s32[18]{0:T(128)} %pad_add_fusion.ints, f32[4]{0:T(128)} %pad_maximum_fusion.5.floats, f32[3,2,16,64,256]{4,3,2,1,0:T(8,128)} %vel.3, bf16[256,512]{1,0:T(8,128)(2,1)} %constant.43.clone.yh, ...), custom_call_target="tpu_custom_call" | custom-call | tf_op jit(solution)/shard_map/head/pallas_call | solution.py:417
  17.6 32.0 %all_to_all.35 = f32[8,4,16,8,128]{4,3,2,1,0:T(8,128)} all-to-all(f32[8,4,16,8,128]{4,3,2,1,0:T(8,128)} %get-tuple-element.29), channel_id=1, replica_groups=mesh['row'=8,'col'=4] {'row'}, dimensions={0} | all-to-all | bytes 4194304 | tf_op jit(solution)/shard_map/all_to_all | solution.py:639
  49.6 29.7 %all_to_all.36 = f32[8,4,16,8,128]{4,3,2,1,0:T(8,128)} all-to-all(f32[8,4,16,8,128]{4,3,2,1,0:T(8,128)S(1)} %copy-done.3), channel_id=1, replica_groups=mesh['row'=8,'col'=4] {'row'}, dimensions={0} | all-to-all | bytes 4194304 | tf_op jit(solution)/shard_map/all_to_all | solution.py:639
  95.3 14.2 %all-to-all-done.3 = f32[8,4,16,8,128]{4,3,2,1,0:T(8,128)S(1)} async-done(((f32[8,4,16,8,128]{4,3,2,1,0:T(8,128)}), f32[8,4,16,8,128]{4,3,2,1,0:T(8,128)S(1)}, u32[]{:S(2)}, u32[]{:S(2)}) %all-to-all-start.3) | async-done | bytes 2097184 | tf_op jit(solution)/shard_map/all_to_all | solution.py:639
  114.6 11.6 %collective-permute-start.2 = (f32[88,8,128]{2,1,0:T(8,128)S(1)}, f32[88,8,128]{2,1,0:T(8,128)S(1)}, u32[]{:S(2)}, u32[]{:S(2)}) collective-permute-start(f32[88,8,128]{2,1,0:T(8,128)S(1)} %slice.111), channel_id=1, source_target_pairs={{0,3},{1,2},{2,1},{3,0},{4,7},{5,6},{6,5},{7,4},{8,11},{9,10},{10,... | collective-permute-start | bytes 1081352 | tf_op jit(solution)/shard_map/ppermute | solution.py:634
  129.1 7.4 %to_grid.4.refs_1_.refs_2_ = f32[8,256,256]{2,1,0:T(8,128)} custom-call(s32[18]{0:T(128)} %pad_add_fusion.ints, f32[88,8,128]{2,1,0:T(8,128)} %slice.113.refs_0_, f32[88,8,128]{2,1,0:T(8,128)} %collective-permute-done.3.refs_1_, f32[88,8,128]{2,1,0:T(8,128)} %collective-permute-done.4.refs_2_, f32[88,8,128]{2,1,0:T(8,128)} %collective-permute-done.5.refs_3_, ...), custom_call_target="tpu_custom_call" | custom-call | tf_op jit(solution)/shard_map/to_grid/pallas_call | solution.py:471
  136.6 26.6 %collective-permute-done.1.refs_2_ = f32[88,8,128]{2,1,0:T(8,128)S(1)} collective-permute-done((f32[88,8,128]{2,1,0:T(8,128)S(1)}, f32[88,8,128]{2,1,0:T(8,128)S(1)}, u32[]{:S(2)}, u32[]{:S(2)}) %collective-permute-start.1) | collective-permute-done | bytes 360480 | tf_op jit(solution)/shard_map/ppermute | solution.py:634
  164.6 7.4 %to_grid.3.refs_0_ = f32[8,256,256]{2,1,0:T(8,128)} custom-call(s32[18]{0:T(128)} %pad_add_fusion.ints, f32[88,8,128]{2,1,0:T(8,128)} %slice.105.refs_0_, f32[88,8,128]{2,1,0:T(8,128)} %collective-permute-done.refs_1_, f32[88,8,128]{2,1,0:T(8,128)} %copy-done.8, f32[88,8,128]{2,1,0:T(8,128)} %copy-done.10, bf16[4,128,512]{2,1,0:T(8,128)(2,1)} %constant.51.clone.refs_4_, ...), custom_call_target="tpu_custom_call" | custom-call | tf_op jit(solution)/shard_map/to_grid/pallas_call | solution.py:471
  180.1 7.5 %to_grid.5.refs_1_.refs_0_ = f32[8,256,256]{2,1,0:T(8,128)} custom-call(s32[18]{0:T(128)} %pad_add_fusion.ints, f32[88,8,128]{2,1,0:T(8,128)} %slice.121.refs_0_, f32[88,8,128]{2,1,0:T(8,128)} %copy-done.6, f32[88,8,128]{2,1,0:T(8,128)} %copy-done.7, f32[88,8,128]{2,1,0:T(8,128)} %copy-done.9, bf16[4,128,512]{2,1,0:T(8,128)(2,1)} %constant.51.clone.refs_4_, ...), custom_call_target="tpu_custom_call" | custom-call | tf_op jit(solution)/shard_map/to_grid/pallas_call | solution.py:471
  187.6 11.1 %shard_map.212 = (f32[88,8,128]{2,1,0:T(8,128)}, f32[88,8,128]{2,1,0:T(8,128)}, f32[88,8,128]{2,1,0:T(8,128)}, f32[88,8,128]{2,1,0:T(8,128)}, f32[88,8,128]{2,1,...) custom-call(s32[18]{0:T(128)} %pad_add_fusion.ints, ...), custom_call_target="tpu_custom_call" | custom-call | tf_op jit(solution)/shard_map/pallas_call | solution.py:562
  198.7 7.6 %collective-permute-start.12 = (f32[88,8,128]{2,1,0:T(8,128)}, f32[88,8,128]{2,1,0:T(8,128)S(1)}, u32[]{:S(2)}, u32[]{:S(2)}) collective-permute-start(f32[88,8,128]{2,1,0:T(8,128)} %get-tuple-element.37), channel_id=1, source_target_pairs={{0,1},{1,0},{2,3},{3,2},{4,5},{5,4},{6,7},{7,6},{8,9},{9,8},{10,11... | collective-permute-start | bytes 1081352 | tf_op jit(solution)/shard_map/ppermute | solution.py:634
  210.7 11.0 %collective-permute-done.12 = f32[88,8,128]{2,1,0:T(8,128)S(1)} collective-permute-done((f32[88,8,128]{2,1,0:T(8,128)}, f32[88,8,128]{2,1,0:T(8,128)S(1)}, u32[]{:S(2)}, u32[]{:S(2)}) %collective-permute-start.12) | collective-permute-done | bytes 360480 | tf_op jit(solution)/shard_map/ppermute | solution.py:634
  221.8 12.4 %collective-permute-done.13 = f32[88,8,128]{2,1,0:T(8,128)S(1)} collective-permute-done((f32[88,8,128]{2,1,0:T(8,128)}, f32[88,8,128]{2,1,0:T(8,128)S(1)}, u32[]{:S(2)}, u32[]{:S(2)}) %collective-permute-start.13) | collective-permute-done | bytes 360480 | tf_op jit(solution)/shard_map/ppermute | solution.py:634
  249.1 13.6 %collective-permute-done.15 = f32[88,8,128]{2,1,0:T(8,128)S(1)} collective-permute-done((f32[88,8,128]{2,1,0:T(8,128)S(1)}, f32[88,8,128]{2,1,0:T(8,128)S(1)}, u32[]{:S(2)}, u32[]{:S(2)}) %collective-permute-start.15) | collective-permute-done | bytes 360480 | tf_op jit(solution)/shard_map/ppermute | solution.py:634
  262.7 11.4 %collective-permute-done.16 = f32[88,8,128]{2,1,0:T(8,128)S(1)} collective-permute-done((f32[88,8,128]{2,1,0:T(8,128)S(1)}, f32[88,8,128]{2,1,0:T(8,128)S(1)}, u32[]{:S(2)}, u32[]{:S(2)}) %collective-permute-start.16) | collective-permute-done | bytes 360480 | tf_op jit(solution)/shard_map/ppermute | solution.py:634
  281.5 10.9 %shard_map.211 = (f32[88,8,128]{2,1,0:T(8,128)}, f32[88,8,128]{2,1,0:T(8,128)}, f32[88,8,128]{2,1,0:T(8,128)}, f32[88,8,128]{2,1,0:T(8,128)}, f32[88,8,128]{2,1,...) custom-call(s32[18]{0:T(128)} %pad_add_fusion.ints, ...), custom_call_target="tpu_custom_call" | custom-call | tf_op jit(solution)/shard_map/pallas_call | solution.py:562
  303.3 12.9 %collective-permute-done.6 = f32[88,8,128]{2,1,0:T(8,128)S(1)} collective-permute-done((f32[88,8,128]{2,1,0:T(8,128)}, f32[88,8,128]{2,1,0:T(8,128)S(1)}, u32[]{:S(2)}, u32[]{:S(2)}) %collective-permute-start.6) | collective-permute-done | bytes 360480 | tf_op jit(solution)/shard_map/ppermute | solution.py:634
  316.2 11.5 %collective-permute-done.7 = f32[88,8,128]{2,1,0:T(8,128)S(1)} collective-permute-done((f32[88,8,128]{2,1,0:T(8,128)}, f32[88,8,128]{2,1,0:T(8,128)S(1)}, u32[]{:S(2)}, u32[]{:S(2)}) %collective-permute-start.7) | collective-permute-done | bytes 360480 | tf_op jit(solution)/shard_map/ppermute | solution.py:634
  333.3 8.3 %shard_map.213 = (f32[88,8,128]{2,1,0:T(8,128)}, f32[88,8,128]{2,1,0:T(8,128)}, f32[88,8,128]{2,1,0:T(8,128)}, f32[88,8,128]{2,1,0:T(8,128)}) custom-call(s32[18]{0:T(128)} %pad_add_fusion.ints, f32[8,256,256]{2,1,0:T(8,128)} %to_grid.5.refs_1_.refs_0_, f32[8,256,256]{2,1,0:T(8,128)} %to_grid.4.refs_1_.refs_2_, f32[88,8,128]{2,1,0:T(8,128)} %get-tuple-element.44.refs_2_, ...), custom_call_target="tpu_custom_call" | custom-call | tf_op jit(solution)/shard_map/pallas_call | solution.py:562
  352.2 13.1 %collective-permute-done.18 = f32[88,8,128]{2,1,0:T(8,128)S(1)} collective-permute-done((f32[88,8,128]{2,1,0:T(8,128)}, f32[88,8,128]{2,1,0:T(8,128)S(1)}, u32[]{:S(2)}, u32[]{:S(2)}) %collective-permute-start.18) | collective-permute-done | bytes 360480 | tf_op jit(solution)/shard_map/ppermute | solution.py:634
  365.4 11.3 %collective-permute-done.19 = f32[88,8,128]{2,1,0:T(8,128)S(1)} collective-permute-done((f32[88,8,128]{2,1,0:T(8,128)}, f32[88,8,128]{2,1,0:T(8,128)S(1)}, u32[]{:S(2)}, u32[]{:S(2)}) %collective-permute-start.19) | collective-permute-done | bytes 360480 | tf_op jit(solution)/shard_map/ppermute | solution.py:634
  384.1 16.0 %psum.7 = f32[16,2]{1,0:T(8,128)S(1)} all-reduce(f32[16,2]{1,0:T(8,128)S(1)} %reduce_sum.9), channel_id=1, replica_groups=mesh['row'=8,'col'=4] {'col'}, use_global_device_ids=true, to_apply=%region_1.2 | all-reduce | flops 32 | bytes 256 | tf_op jit(solution)/shard_map/psum | solution.py:674
  400.9 9.7 %all-to-all-done.6.ff = f32[8,4,16,8,128]{4,3,2,1,0:T(8,128)} async-done(((f32[8,4,16,8,128]{4,3,2,1,0:T(8,128)}), f32[8,4,16,8,128]{4,3,2,1,0:T(8,128)}, u32[]{:S(2)}, u32[]{:S(2)}) %all-to-all-start.6) | async-done | bytes 2097184 | tf_op jit(solution)/shard_map/all_to_all | solution.py:639
  410.6 21.8 %tail.1 = (f32[3,2,16,64,256]{4,3,2,1,0:T(8,128)}, f32[3,2,16,64,256]{4,3,2,1,0:T(8,128)}) custom-call(s32[18]{0:T(128)} %pad_add_fusion.ints, f32[4]{0:T(128)} %pad_maximum_fusion.5.floats, f32[3,2,16,64,256]{4,3,2,1,0:T(8,128)} %vel.3, f32[3,2,16,64,256]{4,3,2,1,0:T(8,128)} %acc.1, f32[8,4,16,8,128]{4,3,2,1,0:T(8,128)} %copy-done.2, ...), custom_call_target="tpu_custom_call" | custom-call | tf_op jit(solution)/shard_map/tail/pallas_call | solution.py:620
  (111 shorter events, 97.5 us)
Async XLA Ops:
  79.3 30.2 %all-to-all-start.3 = ((f32[8,4,16,8,128]{4,3,2,1,0:T(8,128)}), f32[8,4,16,8,128]{4,3,2,1,0:T(8,128)S(1)}, u32[]{:S(2)}, u32[]{:S(2)}) async-start(f32[8,4,16,8,128]{4,3,2,1,0:T(8,128)} %get-tuple-element.35), calls=%async_computation.3 | async-start | bytes 4194304 | tf_op jit(solution)/shard_map/all_to_all | solution.py:639
  87.3 24.7 %collective-permute-start = (f32[88,8,128]{2,1,0:T(8,128)}, f32[88,8,128]{2,1,0:T(8,128)}, u32[]{:S(2)}, u32[]{:S(2)}) collective-permute-start(f32[88,8,128]{2,1,0:T(8,128)} %slice.107), channel_id=1, source_target_pairs={{0,1},{1,0},{2,3},{3,2},{4,5},{5,4},{6,7},{7,6},{8,9},{9,8},{10,11... | collective-permute-start | bytes 1081352 | tf_op jit(solution)/shard_map/ppermute | solution.py:634
  89.4 25.2 %collective-permute-start.3 = (f32[88,8,128]{2,1,0:T(8,128)}, f32[88,8,128]{2,1,0:T(8,128)}, u32[]{:S(2)}, u32[]{:S(2)}) collective-permute-start(f32[88,8,128]{2,1,0:T(8,128)} %slice.115), channel_id=1, source_target_pairs={{0,1},{1,0},{2,3},{3,2},{4,5},{5,4},{6,7},{7,6},{8,9},{9,8},{10,11... | collective-permute-start | bytes 1081352 | tf_op jit(solution)/shard_map/ppermute | solution.py:634
  89.4 36.8 %collective-permute-start.4 = (f32[88,8,128]{2,1,0:T(8,128)}, f32[88,8,128]{2,1,0:T(8,128)}, u32[]{:S(2)}, u32[]{:S(2)}) collective-permute-start(f32[88,8,128]{2,1,0:T(8,128)} %slice.117), channel_id=1, source_target_pairs={{0,2},{1,3},{2,0},{3,1},{4,6},{5,7},{6,4},{7,5},{8,10},{9,11},{10,... | collective-permute-start | bytes 1081352 | tf_op jit(solution)/shard_map/ppermute | solution.py:634
  93.2 33.0 %collective-permute-start.5 = (f32[88,8,128]{2,1,0:T(8,128)}, f32[88,8,128]{2,1,0:T(8,128)}, u32[]{:S(2)}, u32[]{:S(2)}) collective-permute-start(f32[88,8,128]{2,1,0:T(8,128)} %slice.119), channel_id=1, source_target_pairs={{0,3},{1,2},{2,1},{3,0},{4,7},{5,6},{6,5},{7,4},{8,11},{9,10},{10,... | collective-permute-start | bytes 1081352 | tf_op jit(solution)/shard_map/ppermute | solution.py:634
  109.8 62.3 %collective-permute-start.9 = (f32[88,8,128]{2,1,0:T(8,128)S(1)}, f32[88,8,128]{2,1,0:T(8,128)S(1)}, u32[]{:S(2)}, u32[]{:S(2)}) collective-permute-start(f32[88,8,128]{2,1,0:T(8,128)S(1)} %slice.123), channel_id=1, source_target_pairs={{0,1},{1,0},{2,3},{3,2},{4,5},{5,4},{6,7},{7,6},{8,9},{9,8},{10,11... | collective-permute-start | bytes 1081352 | tf_op jit(solution)/shard_map/ppermute | solution.py:634
  112.0 51.2 %collective-permute-start.1 = (f32[88,8,128]{2,1,0:T(8,128)S(1)}, f32[88,8,128]{2,1,0:T(8,128)S(1)}, u32[]{:S(2)}, u32[]{:S(2)}) collective-permute-start(f32[88,8,128]{2,1,0:T(8,128)S(1)} %copy-done.4), channel_id=1, source_target_pairs={{0,2},{1,3},{2,0},{3,1},{4,6},{5,7},{6,4},{7,5},{8,10},{9,11},{10,... | collective-permute-start | bytes 1081352 | tf_op jit(solution)/shard_map/ppermute | solution.py:634
  114.6 48.6 %collective-permute-start.2 = (f32[88,8,128]{2,1,0:T(8,128)S(1)}, f32[88,8,128]{2,1,0:T(8,128)S(1)}, u32[]{:S(2)}, u32[]{:S(2)}) collective-permute-start(f32[88,8,128]{2,1,0:T(8,128)S(1)} %slice.111), channel_id=1, source_target_pairs={{0,3},{1,2},{2,1},{3,0},{4,7},{5,6},{6,5},{7,4},{8,11},{9,10},{10,... | collective-permute-start | bytes 1081352 | tf_op jit(solution)/shard_map/ppermute | solution.py:634
  126.2 52.4 %collective-permute-start.10 = (f32[88,8,128]{2,1,0:T(8,128)S(1)}, f32[88,8,128]{2,1,0:T(8,128)S(1)}, u32[]{:S(2)}, u32[]{:S(2)}) collective-permute-start(f32[88,8,128]{2,1,0:T(8,128)S(1)} %slice.125), channel_id=1, source_target_pairs={{0,2},{1,3},{2,0},{3,1},{4,6},{5,7},{6,4},{7,5},{8,10},{9,11},{10,... | collective-permute-start | bytes 1081352 | tf_op jit(solution)/shard_map/ppermute | solution.py:634
  126.2 52.4 %collective-permute-start.11 = (f32[88,8,128]{2,1,0:T(8,128)S(1)}, f32[88,8,128]{2,1,0:T(8,128)S(1)}, u32[]{:S(2)}, u32[]{:S(2)}) collective-permute-start(f32[88,8,128]{2,1,0:T(8,128)S(1)} %slice.127), channel_id=1, source_target_pairs={{0,3},{1,2},{2,1},{3,0},{4,7},{5,6},{6,5},{7,4},{8,11},{9,10},{10,... | collective-permute-start | bytes 1081352 | tf_op jit(solution)/shard_map/ppermute | solution.py:634
  206.3 27.8 %collective-permute-start.13 = (f32[88,8,128]{2,1,0:T(8,128)}, f32[88,8,128]{2,1,0:T(8,128)S(1)}, u32[]{:S(2)}, u32[]{:S(2)}) collective-permute-start(f32[88,8,128]{2,1,0:T(8,128)} %get-tuple-element.38), channel_id=1, source_target_pairs={{0,2},{1,3},{2,0},{3,1},{4,6},{5,7},{6,4},{7,5},{8,10},{9,11},{10,... | collective-permute-start | bytes 1081352 | tf_op jit(solution)/shard_map/ppermute | solution.py:634
  208.3 25.9 %collective-permute-start.14 = (f32[88,8,128]{2,1,0:T(8,128)}, f32[88,8,128]{2,1,0:T(8,128)S(1)}, u32[]{:S(2)}, u32[]{:S(2)}) collective-permute-start(f32[88,8,128]{2,1,0:T(8,128)} %get-tuple-element.39), channel_id=1, source_target_pairs={{0,3},{1,2},{2,1},{3,0},{4,7},{5,6},{6,5},{7,4},{8,11},{9,10},{10,... | collective-permute-start | bytes 1081352 | tf_op jit(solution)/shard_map/ppermute | solution.py:634
  235.7 40.0 %all-to-all-start.4 = ((f32[8,4,16,8,128]{4,3,2,1,0:T(8,128)}), f32[8,4,16,8,128]{4,3,2,1,0:T(8,128)S(1)}, u32[]{:S(2)}, u32[]{:S(2)}) async-start(f32[8,4,16,8,128]{4,3,2,1,0:T(8,128)} %pad_maximum_fusion.1), calls=%async_computation.4 | async-start | bytes 4194304 | tf_op jit(solution)/shard_map/all_to_all | solution.py:639
  246.4 27.7 %collective-permute-start.16 = (f32[88,8,128]{2,1,0:T(8,128)S(1)}, f32[88,8,128]{2,1,0:T(8,128)S(1)}, u32[]{:S(2)}, u32[]{:S(2)}) collective-permute-start(f32[88,8,128]{2,1,0:T(8,128)S(1)} %copy-done.13), channel_id=1, source_target_pairs={{0,2},{1,3},{2,0},{3,1},{4,6},{5,7},{6,4},{7,5},{8,10},{9,11},{10,... | collective-permute-start | bytes 1081352 | tf_op jit(solution)/shard_map/ppermute | solution.py:634
  247.6 26.5 %collective-permute-start.17 = (f32[88,8,128]{2,1,0:T(8,128)S(1)}, f32[88,8,128]{2,1,0:T(8,128)S(1)}, u32[]{:S(2)}, u32[]{:S(2)}) collective-permute-start(f32[88,8,128]{2,1,0:T(8,128)S(1)} %copy-done.12), channel_id=1, source_target_pairs={{0,3},{1,2},{2,1},{3,0},{4,7},{5,6},{6,5},{7,4},{8,11},{9,10},{10,... | collective-permute-start | bytes 1081352 | tf_op jit(solution)/shard_map/ppermute | solution.py:634
  277.1 52.1 %all-to-all-start.5 = ((f32[8,4,16,8,128]{4,3,2,1,0:T(8,128)}), f32[8,4,16,8,128]{4,3,2,1,0:T(8,128)}, u32[]{:S(2)}, u32[]{:S(2)}) async-start(f32[8,4,16,8,128]{4,3,2,1,0:T(8,128)} %pad_maximum_fusion.2), calls=%async_computation.5 | async-start | bytes 4194304 | tf_op jit(solution)/shard_map/all_to_all | solution.py:639
  292.4 23.8 %collective-permute-start.6 = (f32[88,8,128]{2,1,0:T(8,128)}, f32[88,8,128]{2,1,0:T(8,128)S(1)}, u32[]{:S(2)}, u32[]{:S(2)}) collective-permute-start(f32[88,8,128]{2,1,0:T(8,128)} %get-tuple-element.32), channel_id=1, source_target_pairs={{0,1},{1,0},{2,3},{3,2},{4,5},{5,4},{6,7},{7,6},{8,9},{9,8},{10,11... | collective-permute-start | bytes 1081352 | tf_op jit(solution)/shard_map/ppermute | solution.py:634
  299.8 27.9 %collective-permute-start.7 = (f32[88,8,128]{2,1,0:T(8,128)}, f32[88,8,128]{2,1,0:T(8,128)S(1)}, u32[]{:S(2)}, u32[]{:S(2)}) collective-permute-start(f32[88,8,128]{2,1,0:T(8,128)} %get-tuple-element.33), channel_id=1, source_target_pairs={{0,2},{1,3},{2,0},{3,1},{4,6},{5,7},{6,4},{7,5},{8,10},{9,11},{10,... | collective-permute-start | bytes 1081352 | tf_op jit(solution)/shard_map/ppermute | solution.py:634
  300.9 26.8 %collective-permute-start.8 = (f32[88,8,128]{2,1,0:T(8,128)}, f32[88,8,128]{2,1,0:T(8,128)S(1)}, u32[]{:S(2)}, u32[]{:S(2)}) collective-permute-start(f32[88,8,128]{2,1,0:T(8,128)} %get-tuple-element.34), channel_id=1, source_target_pairs={{0,3},{1,2},{2,1},{3,0},{4,7},{5,6},{6,5},{7,4},{8,11},{9,10},{10,... | collective-permute-start | bytes 1081352 | tf_op jit(solution)/shard_map/ppermute | solution.py:634
  329.3 48.9 %all-to-all-start.2 = ((f32[8,4,16,8,128]{4,3,2,1,0:T(8,128)}), f32[8,4,16,8,128]{4,3,2,1,0:T(8,128)S(1)}, u32[]{:S(2)}, u32[]{:S(2)}) async-start(f32[8,4,16,8,128]{4,3,2,1,0:T(8,128)} %pad_maximum_fusion), calls=%async_computation.2 | async-start | bytes 4194304 | tf_op jit(solution)/shard_map/all_to_all | solution.py:639
  341.6 23.7 %collective-permute-start.18 = (f32[88,8,128]{2,1,0:T(8,128)}, f32[88,8,128]{2,1,0:T(8,128)S(1)}, u32[]{:S(2)}, u32[]{:S(2)}) collective-permute-start(f32[88,8,128]{2,1,0:T(8,128)} %get-tuple-element.49), channel_id=1, source_target_pairs={{0,1},{1,0},{2,3},{3,2},{4,5},{5,4},{6,7},{7,6},{8,9},{9,8},{10,11... | collective-permute-start | bytes 1081352 | tf_op jit(solution)/shard_map/ppermute | solution.py:634
  348.7 27.9 %collective-permute-start.19 = (f32[88,8,128]{2,1,0:T(8,128)}, f32[88,8,128]{2,1,0:T(8,128)S(1)}, u32[]{:S(2)}, u32[]{:S(2)}) collective-permute-start(f32[88,8,128]{2,1,0:T(8,128)} %get-tuple-element.50), channel_id=1, source_target_pairs={{0,2},{1,3},{2,0},{3,1},{4,6},{5,7},{6,4},{7,5},{8,10},{9,11},{10,... | collective-permute-start | bytes 1081352 | tf_op jit(solution)/shard_map/ppermute | solution.py:634
  349.8 26.9 %collective-permute-start.20 = (f32[88,8,128]{2,1,0:T(8,128)}, f32[88,8,128]{2,1,0:T(8,128)S(1)}, u32[]{:S(2)}, u32[]{:S(2)}) collective-permute-start(f32[88,8,128]{2,1,0:T(8,128)} %get-tuple-element.51), channel_id=1, source_target_pairs={{0,3},{1,2},{2,1},{3,0},{4,7},{5,6},{6,5},{7,4},{8,11},{9,10},{10,... | collective-permute-start | bytes 1081352 | tf_op jit(solution)/shard_map/ppermute | solution.py:634
  379.6 31.0 %all-to-all-start.6 = ((f32[8,4,16,8,128]{4,3,2,1,0:T(8,128)}), f32[8,4,16,8,128]{4,3,2,1,0:T(8,128)}, u32[]{:S(2)}, u32[]{:S(2)}) async-start(f32[8,4,16,8,128]{4,3,2,1,0:T(8,128)} %pad_maximum_fusion.3), calls=%async_computation.6 | async-start | bytes 4194304 | tf_op jit(solution)/shard_map/all_to_all | solution.py:639
  (17 other events, 141.7 us)
where the time goes:
time: 438 us; the launch traced here: 432 us
  waiting for transfers between devices  154 us (35%)
  Pallas kernels  86.8 us (20%)
  starting transfers between devices  83.7 us (19%)
  blocking collectives  77.8 us (18%)
  local copies, waits for them, and re-layouts  17.7 us (4%)
  other arithmetic  8.81 us (2%)
    ppermute x21, waiting for transfers between devices, col_exchange(): lax.ppermute(pieces[q], 'col', [(i, i ^ q) for i in range(s.cols)])  130 us
    ppermute x21, starting transfers between devices, col_exchange(): lax.ppermute(pieces[q], 'col', [(i, i ^ q) for i in range(s.cols)])  63.4 us
    all_to_all x2, blocking collectives, row_exchange(): return lax.all_to_all(field, 'row', 0, 0, tiled=True)  61.7 us
    pallas_call x3, Pallas kernels, products(): pl.pallas_call(functools.partial(back_kernel, s, which), in_specs=[pl.Blo...  30.3 us
    all_to_all x5, waiting for transfers between devices, row_exchange(): return lax.all_to_all(field, 'row', 0, 0, tiled=True)  23.9 us
    pallas_call x3, Pallas kernels, to_grid(): pl.pallas_call(functools.partial(grid_kernel, s), in_specs=[pl.BlockSpec(...  22.3 us
    pallas_call x1, Pallas kernels, tail(): pl.pallas_call(functools.partial(tail_kernel, s), grid=(s.width_x,), in_s...  21.8 us
    all_to_all x5, starting transfers between devices, row_exchange(): return lax.all_to_all(field, 'row', 0, 0, tiled=True)  20.3 us
  transfers between devices with their start and end apart: 26, of which 12 were waited for; matrix products, arithmetic and copies ran while one was open for 4% of the time, Pallas kernels for 8%

commit v1 on v0

--- a/solution.py
+++ b/solution.py
@@ -296,7 +296,7 @@
     table = np.asarray(table, np.float32)
     high = table.astype(jnp.bfloat16)
     low = (table - high.astype(np.float32)).astype(jnp.bfloat16)
-    return jnp.asarray(high), jnp.asarray(low)
+    return high, low
 
 
 def split(x):
@@ -324,6 +324,7 @@
     def fits(self):
         return (
             self.block_y == 8
+            and self.cols == 4
             and self.lanes == 128
             and self.full_y % 128 == 0
             and self.full_z % 128 == 0
@@ -352,7 +353,20 @@
     z_fore = np.concatenate(
         [np.concatenate([ct, -nt], axis=2), np.concatenate([nt, ct], axis=2)], axis=1
     )
-    return [halves(t) for t in (y_back, y_fore, x_back, x_fore, z_back, z_fore)]
+    left = [np.concatenate(halves(t), axis=0) for t in (y_back, x_back, x_fore)]
+    return left + [halves(t) for t in (y_fore, z_back, z_fore)]
+
+
+def by_left_table(table, rows, high, low, inner):
+    out = dot(table[...], high, inner)
+    return out[:rows] + (out[rows:] + dot(table[:rows], low, inner))
+
+
+def by_right_table(data, high, low):
+    n = data.shape[0]
+    top, rest = split(data)
+    out = dot(jnp.concatenate([top, rest], axis=0), high, ((1,), (0,)))
+    return out[:n] + (out[n:] + dot(top, low, ((1,), (0,))))
 
 
 def whole(shape):
@@ -381,8 +395,8 @@
     return [[flat[(2 * c + p) * w : (2 * c + p + 1) * w] for p in range(2)] for c in range(3)]
 
 
-def head_kernel(s, ints, floats, vel, yh, yl, *outs):
-    fields, sums = outs[:3], outs[3]
+def head_kernel(s, ints, floats, vel, table, *outs):
+    fields, sums, made = outs[:-2], outs[-2], outs[-1]
     row, col = ints[0], ints[1]
     step = pl.program_id(0)
     right = [[], [], []]
@@ -399,68 +413,69 @@
         along = [(k0 * v[0][p] + k1 * v[1][p] + k2 * v[2][p]) * inverse for p in range(2)]
         for c, k in enumerate((k0, k1, k2)):
             (rh, rl), (ih, il) = [split(mask * (v[c][p] - k * along[p])) for p in range(2)]
-            right[c].append(jnp.concatenate([rh, ih, rl, il, rh, ih], axis=1))
-            right[c].append(jnp.concatenate([ih, -rh, il, -rl, ih, -rh], axis=1))
-    left = jnp.concatenate([yh[...], yh[...], yl[...]], axis=1)
+            right[c].append([jnp.concatenate([rh, ih], axis=1), jnp.concatenate([rl, il], axis=1)])
+            right[c].append([jnp.concatenate([ih, -rh], axis=1), jnp.concatenate([il, -rl], axis=1)])
     for c in range(3):
-        out = dot(left, jnp.concatenate(right[c], axis=0), ((1,), (1,)))
+        high, low = [jnp.concatenate([x[i] for x in right[c]], axis=0) for i in range(2)]
+        made[...] = by_left_table(table, s.full_y, high, low, ((1,), (1,)))
         for r in range(s.rows):
             for q in range(s.cols):
-                at = (r * s.cols + q) * 8
+                at = pl.multiple_of((r * s.cols + (q ^ col)) * 8, 8)
                 for j in range(2):
-                    fields[c][r, q ^ col, j] = out[at : at + 8, j * 128 : (j + 1) * 128]
+                    tile = made[pl.ds(at, 8), j * 128 : (j + 1) * 128]
+                    if c < 2:
+                        fields[c][r, q, j] = tile
+                    else:
+                        fields[c + q][r, j] = tile
 
 
 def head(s, ints, floats, velocity, table):
-    y2 = (s.full_y, 2 * s.full_y)
-    piece = (s.rows, s.cols, s.width_x, 8, s.lanes)
-    return pl.pallas_call(
+    out = pl.pallas_call(
         functools.partial(head_kernel, s),
         grid=(s.width_x // 2,),
         in_specs=[
             pl.BlockSpec(memory_space=pltpu.SMEM),
             pl.BlockSpec(memory_space=pltpu.SMEM),
             pl.BlockSpec((3, 2, 2, s.width_z, s.full_y), lambda i: (0, 0, i, 0, 0)),
-            whole(y2),
-            whole(y2),
+            whole(table.shape),
         ],
-        out_specs=[pl.BlockSpec((s.rows, s.cols, 2, 8, s.lanes), lambda i: (0, 0, i, 0, 0))] * 3
+        out_specs=[pl.BlockSpec((s.rows, s.cols, 2, 8, s.lanes), lambda i: (0, 0, i, 0, 0))] * 2
+        + [pl.BlockSpec((s.rows, 2, 8, s.lanes), lambda i: (0, i, 0, 0))] * s.cols
         + [pl.BlockSpec((2, 2, 8, s.full_y), lambda i: (i, 0, 0, 0))],
-        out_shape=[jax.ShapeDtypeStruct(piece, F32)] * 3
+        out_shape=[jax.ShapeDtypeStruct((s.rows, s.cols, s.width_x, 8, s.lanes), F32)] * 2
+        + [jax.ShapeDtypeStruct((s.rows, s.width_x, 8, s.lanes), F32)] * s.cols
         + [jax.ShapeDtypeStruct((s.width_x, 2, 8, s.full_y), F32)],
+        scratch_shapes=[pltpu.VMEM((s.full_y, 256), F32)],
         compiler_params=pltpu.CompilerParams(vmem_limit_bytes=VMEM_LIMIT),
         name="head",
-    )(ints, floats, velocity, *table)
+    )(ints, floats, velocity, table)
+    return out[0], out[1], out[2:-1], out[-1]
 
 
 def grid_kernel(s, ints, *refs):
-    pieces, (zh, zl, xh, xl, out, mid) = refs[: s.cols], refs[s.cols :]
+    pieces, (zh, zl, x_table, out, mid) = refs[: s.cols], refs[s.cols :]
     col = ints[1]
     rows = s.live_x * 8
-    step = rows // 4
-    zt = jnp.concatenate(
-        [zh[q ^ col] for q in range(s.cols)] * 2 + [zl[q ^ col] for q in range(s.cols)], axis=0
-    )
+    step = rows // 2
+    high_z = jnp.concatenate([zh[q ^ col] for q in range(s.cols)], axis=0)
+    low_z = jnp.concatenate([zl[q ^ col] for q in range(s.cols)], axis=0)
 
     def along_z(i, carry):
         at = pl.multiple_of(i * (step // 8), step // 8)
-        parts = [split(p[pl.ds(at, step // 8)].reshape(step, s.lanes)) for p in pieces]
-        highs, lows = [h for h, _ in parts], [l for _, l in parts]
-        left = jnp.concatenate(highs + lows + highs, axis=1)
-        full = dot(left, zt, ((1,), (0,)))
+        parts = [p[pl.ds(at, step // 8)].reshape(step, s.lanes) for p in pieces]
+        full = by_right_table(jnp.concatenate(parts, axis=1), high_z, low_z)
         for t in range(2 * s.full_z // 128):
             mid[t, pl.ds(pl.multiple_of(i * step, step), step)] = full[:, t * 128 : (t + 1) * 128]
         return carry
 
-    lax.fori_loop(0, 4, along_z, 0)
-    xt = jnp.concatenate([xh[...], xh[...], xl[...]], axis=1)
+    lax.fori_loop(0, 2, along_z, 0)
 
     def along_x(y, carry):
         tiles = [mid[t, pl.ds(y, s.live_x, stride=8)] for t in range(2 * s.full_z // 128)]
         half = s.full_z // 128
         both = [jnp.concatenate(tiles[:half], axis=1), jnp.concatenate(tiles[half:], axis=1)]
         high, low = split(jnp.concatenate(both, axis=0))
-        out[y] = dot(xt, jnp.concatenate([high, low, high], axis=0), ((1,), (0,)))
+        out[y] = by_left_table(x_table, s.full_x, high, low, ((1,), (0,)))
         return carry
 
     lax.fori_loop(0, 8, along_x, 0)
@@ -471,13 +486,13 @@
     return pl.pallas_call(
         functools.partial(grid_kernel, s),
         in_specs=[pl.BlockSpec(memory_space=pltpu.SMEM)]
-        + [pl.BlockSpec(memory_space=pltpu.VMEM)] * (s.cols + 4),
+        + [pl.BlockSpec(memory_space=pltpu.VMEM)] * (s.cols + 3),
         out_specs=pl.BlockSpec(memory_space=pltpu.VMEM),
         out_shape=jax.ShapeDtypeStruct((8, s.full_x, s.full_z), F32),
         scratch_shapes=[pltpu.VMEM((2 * s.full_z // 128, rows, 128), F32)],
         compiler_params=pltpu.CompilerParams(vmem_limit_bytes=VMEM_LIMIT),
         name="to_grid",
-    )(ints, *pieces, *z_table, *x_table)
+    )(ints, *pieces, *z_table, x_table)
 
 
 def turn(s, rows, base, kz):
@@ -491,10 +506,9 @@
     given, _, made = BACK[which]
     u, refs = refs[:given], refs[given:]
     saved, refs = (refs[: s.cols], refs[s.cols :]) if which == 2 else (None, refs)
-    (xh, xl, zh, zl), refs = refs[:4], refs[4:]
+    (x_table, zh, zl), refs = refs[:3], refs[3:]
     outs, mids = refs[: made * s.cols], refs[made * s.cols :]
     col = ints[1]
-    xt = jnp.concatenate([xh[...], xh[...], xl[...]], axis=1)
 
     def along_x(y, carry):
         w = [ref[y] for ref in u]
@@ -506,7 +520,7 @@
             terms = [w[0] * w[0] - w[1] * w[1]]
         for mid, term in zip(mids, terms):
             high, low = split(term)
-            out = dot(xt, jnp.concatenate([high, low, high], axis=0), ((1,), (0,)))
+            out = by_left_table(x_table, 2 * s.live_x, high, low, ((1,), (0,)))
             half = s.full_z // 128
             for t in range(2 * half):
                 p, at = t // half, (t % half) * 128
@@ -516,18 +530,16 @@
 
     lax.fori_loop(0, 8, along_x, 0)
     rows = s.live_x * 8
-    step = rows // 4
-    zt = [jnp.concatenate([zh[q ^ col], zh[q ^ col], zl[q ^ col]], axis=0) for q in range(s.cols)]
-    zt = jnp.concatenate(zt, axis=1)
+    step = rows // 2
+    high_z = jnp.concatenate([zh[q ^ col] for q in range(s.cols)], axis=1)
+    low_z = jnp.concatenate([zl[q ^ col] for q in range(s.cols)], axis=1)
 
     def along_z(i, carry):
         at = pl.multiple_of(i * step, step)
         done = []
         for mid in mids:
-            high, low = split(
-                jnp.concatenate([mid[t, pl.ds(at, step)] for t in range(2 * s.full_z // 128)], axis=1)
-            )
-            done.append(dot(jnp.concatenate([high, low, high], axis=1), zt, ((1,), (0,))))
+            data = [mid[t, pl.ds(at, step)] for t in range(2 * s.full_z // 128)]
+            done.append(by_right_table(jnp.concatenate(data, axis=1), high_z, low_z))
         here = pl.ds(pl.multiple_of(i * (step // 8), step // 8), step // 8)
         shape = (step // 8, 8, s.lanes)
         for q in range(s.cols):
@@ -549,7 +561,7 @@
             outs[s.cols + q][here] = second.reshape(shape)
         return carry
 
-    lax.fori_loop(0, 4, along_z, 0)
+    lax.fori_loop(0, 2, along_z, 0)
 
 
 BACK = ((2, 2, 2), (3, 2, 2), (2, 1, 1))
@@ -562,49 +574,56 @@
     out = pl.pallas_call(
         functools.partial(back_kernel, s, which),
         in_specs=[pl.BlockSpec(memory_space=pltpu.SMEM)]
-        + [pl.BlockSpec(memory_space=pltpu.VMEM)] * (len(fields) + 4),
+        + [pl.BlockSpec(memory_space=pltpu.VMEM)] * (len(fields) + 3),
         out_specs=[pl.BlockSpec(memory_space=pltpu.VMEM)] * (made * s.cols),
         out_shape=[piece] * (made * s.cols),
         scratch_shapes=[pltpu.VMEM((2 * s.full_z // 128, rows, 128), F32)] * number,
         compiler_params=pltpu.CompilerParams(vmem_limit_bytes=VMEM_LIMIT),
-    )(ints, *fields, *x_table, *z_table)
+    )(ints, *fields, x_table, *z_table)
     return [out[i * s.cols : (i + 1) * s.cols] for i in range(made)]
 
 
-def tail_kernel(s, ints, floats, vel, acc, fa, fb, fc, ff, yh, yl, new_vel, new_acc):
-    row, col = ints[0], ints[1]
-    local = pl.program_id(0)
-    kx = row * s.width_x + local
-    amount = ints[2 + local]
-    right = jnp.concatenate([yh[...], yh[...], yl[...]], axis=0)
-    modes = []
-    for ref in (fa, fb, fc, ff):
-        tiles = [ref[r, q ^ col, 0] for r in range(s.rows) for q in range(s.cols)]
-        high, low = split(jnp.concatenate(tiles, axis=0).T)
-        both = dot(jnp.concatenate([high, low, high], axis=1), right, ((1,), (0,)))
-        w, n = s.width_z, s.full_y
-        modes.append((both[:w, :n] + both[w:, n:], both[w:, :n] - both[:w, n:]))
-    k0, k1, k2, ksq, inverse, mask = waves(s, kx, col, floats[0])
+def frame(s, kx, col, shear_clock):
+    k0, k1, k2, ksq, inverse, mask = waves(s, kx, col, shear_clock)
     flat = k0 * k0 + k2 * k2
     scale = lax.rsqrt(jnp.maximum(flat, 1.0))
     cosine, sine = jnp.where(flat > 0, k0 * scale, 1.0), k2 * scale
-    kh = flat * scale
-    lean = (flat - k1 * k1) * inverse
-    cross = kh * k1 * inverse
+    return (k0, k1, k2), ksq, inverse, mask, flat, flat * scale, cosine, sine
+
+
+def modes_of(s, col, refs, yh, yl):
+    turned = []
+    for ref in refs:
+        tiles = [ref[r, q ^ col, 0] for r in range(s.rows) for q in range(s.cols)]
+        turned.append(jnp.concatenate(tiles, axis=0).T)
+    every = by_right_table(jnp.concatenate(turned, axis=0), yh[...], yl[...])
+    modes = []
+    w, n = s.width_z, s.full_y
+    for i in range(len(refs)):
+        both = every[i * s.lanes : (i + 1) * s.lanes]
+        modes.append((both[:w, :n] + both[w:, n:], both[w:, :n] - both[:w, n:]))
+    return modes
+
+
+def early_kernel(s, ints, floats, vel, acc, fa, fb, yh, yl, new_vel, new_acc):
+    row, col = ints[0], ints[1]
+    local = pl.program_id(0)
+    kx, amount = row * s.width_x + local, ints[2 + local]
+    modes = modes_of(s, col, (fa, fb), yh, yl)
+    k, ksq, inverse, mask, _, kh, cosine, sine = frame(s, kx, col, floats[0])
     v = rolled(s, vel, 0, amount)
     old = rolled(s, acc, 0, amount)
     shear, viscosity, dt = floats[1], floats[2], floats[3]
-    coupling = (2.0 * shear) * k0 * inverse
+    coupling = (2.0 * shear) * k[0] * inverse
     for p in range(2):
-        a, b, c, f = [m[1 - p] for m in modes]
-        sign = mask if p == 0 else -mask
-        qt = (kh * a + k1 * b) * sign
-        qe = (lean * c + cross * f) * sign
-        slope = qe * k1
-        nonlinear = (qt * sine - slope * cosine, qe * kh, -(qt * cosine) - slope * sine)
+        a, b = [m[1 - p] for m in modes]
+        qt = (kh * a + k[1] * b) * (mask if p == 0 else -mask)
+        nonlinear = (qt * sine, None, -(qt * cosine))
         drive = coupling * v[1][p]
-        for c3, k in enumerate((k0, k1, k2)):
-            rate = nonlinear[c3] + k * drive - (viscosity * ksq) * v[c3][p]
+        for c3 in range(3):
+            rate = k[c3] * drive - (viscosity * ksq) * v[c3][p]
+            if c3 != 1:
+                rate = rate + nonlinear[c3]
             if c3 == 0:
                 rate = rate - shear * v[1][p]
             fresh = (-5.0 / 9.0) * old[c3][p] + dt * rate
@@ -612,19 +631,41 @@
             new_vel[c3, p, 0] = v[c3][p] + (15.0 / 16.0) * fresh
 
 
-def tail(s, ints, floats, velocity, accumulator, fields, table):
+def late_kernel(s, ints, floats, vel, acc, fc, ff, yh, yl, new_vel, new_acc):
+    row, col = ints[0], ints[1]
+    kx = row * s.width_x + pl.program_id(0)
+    modes = modes_of(s, col, (fc, ff), yh, yl)
+    k, _, inverse, mask, flat, kh, cosine, sine = frame(s, kx, col, floats[0])
+    dt = floats[3] * mask
+    lean = dt * (flat - k[1] * k[1]) * inverse
+    cross = dt * kh * k[1] * inverse
+    for p in range(2):
+        c, f = [m[1 - p] for m in modes]
+        qe = lean * c + cross * f
+        if p == 1:
+            qe = -qe
+        slope = qe * k[1]
+        for c3, add in enumerate((-(slope * cosine), qe * kh, -(slope * sine))):
+            new_acc[c3, p, 0] = acc[c3, p, 0] + add
+            new_vel[c3, p, 0] = vel[c3, p, 0] + (15.0 / 16.0) * add
+
+
+def update(s, kernel, ints, floats, velocity, accumulator, fields, table, alias):
     plane = pl.BlockSpec((3, 2, 1, s.width_z, s.full_y), lambda i: (0, 0, i, 0, 0))
     piece = pl.BlockSpec((s.rows, s.cols, 1, 8, s.lanes), lambda i: (0, 0, i, 0, 0))
     y2 = (s.full_y, 2 * s.full_y)
     shape = jax.ShapeDtypeStruct(velocity.shape, F32)
     return pl.pallas_call(
-        functools.partial(tail_kernel, s),
+        functools.partial(kernel, s),
         grid=(s.width_x,),
-        in_specs=[pl.BlockSpec(memory_space=pltpu.SMEM)] * 2 + [plane] * 2 + [piece] * 4 + [whole(y2)] * 2,
+        in_specs=[pl.BlockSpec(memory_space=pltpu.SMEM)] * 2
+        + [plane] * 2
+        + [piece] * 2
+        + [whole(y2)] * 2,
         out_specs=[plane] * 2,
         out_shape=[shape] * 2,
+        input_output_aliases=alias,
         compiler_params=pltpu.CompilerParams(vmem_limit_bytes=VMEM_LIMIT),
-        name="tail",
     )(ints, floats, velocity, accumulator, *fields, *table)
 
 
@@ -639,44 +680,76 @@
     return lax.all_to_all(field, "row", 0, 0, tiled=True)
 
 
-def forward_field(s, field):
-    got = row_exchange(field)
-    pieces = [
-        got[:, q].reshape(s.half_x, 8, s.lanes)[: s.live_x] for q in range(s.cols)
-    ]
-    return col_exchange(s, pieces)
-
-
-def backward_field(s, pieces):
-    got = col_exchange(s, pieces)
-    spare = ((0, s.half_x - s.live_x), (0, 0), (0, 0))
-    both = jnp.stack(
-        [jnp.pad(p, spare).reshape(s.rows, s.width_x, 8, s.lanes) for p in got], axis=1
-    )
-    return row_exchange(both)
+def of_cols(s, got):
+    return [got[:, q].reshape(s.half_x, 8, s.lanes)[: s.live_x] for q in range(s.cols)]
+
+
+def spread_kernel(s, *refs):
+    pieces, out = refs[:-1], refs[-1]
+    for q, piece in enumerate(pieces):
+        for r in range(s.rows):
+            live = min(max(s.live_x - r * s.width_x, 0), s.width_x)
+            if live:
+                out[r, q, :live] = piece[r * s.width_x : r * s.width_x + live]
+            if live < s.width_x:
+                out[r, q, live:] = jnp.zeros((s.width_x - live, 8, s.lanes), F32)
+
+
+def of_rows(s, pieces):
+    return pl.pallas_call(
+        functools.partial(spread_kernel, s),
+        in_specs=[pl.BlockSpec(memory_space=pltpu.VMEM)] * s.cols,
+        out_specs=pl.BlockSpec(memory_space=pltpu.VMEM),
+        out_shape=jax.ShapeDtypeStruct((s.rows, s.cols, s.width_x, 8, s.lanes), F32),
+        compiler_params=pltpu.CompilerParams(vmem_limit_bytes=VMEM_LIMIT),
+        name="spread",
+    )(*pieces)
+
+
+def forward_rows_first(s, field):
+    return col_exchange(s, of_cols(s, row_exchange(field)))
+
+
+def forward_cols_first(s, pieces):
+    return of_cols(s, row_exchange(jnp.stack(col_exchange(s, pieces), axis=1)))
+
+
+def backward_cols_first(s, pieces):
+    return row_exchange(of_rows(s, col_exchange(s, pieces)))
+
+
+def backward_rows_first(s, pieces):
+    got = row_exchange(of_rows(s, pieces))
+    return jnp.stack(col_exchange(s, [got[:, q] for q in range(s.cols)]), axis=1)
 
 
 def tiled_body(s, velocity, accumulator, remesh_flag, remesh_shift, viscosity, shear, clock, step):
-    y_back, y_fore, x_back, x_fore, z_back, z_fore = constant_tables(s)
+    y_back, x_back, x_fore, y_fore, z_back, z_fore = constant_tables(s)
     place = jnp.stack([lax.axis_index("row"), lax.axis_index("col")]).astype(jnp.int32)
     ints = jnp.concatenate([place, remesh_flag * remesh_shift])
     floats = jnp.concatenate([shear * clock, shear, viscosity, step])
     v0, v1, v2, sums = head(s, ints, floats, velocity, y_back)
 
-    def up(field):
-        return to_grid(s, ints, forward_field(s, field), z_back, x_back)
-
-    u0, u2, u1 = up(v0), up(v2), up(v1)
+    def grid(pieces):
+        return to_grid(s, ints, pieces, z_back, x_back)
+
+    u0 = grid(forward_rows_first(s, v0))
+    u2 = grid(forward_cols_first(s, v2))
+    u1 = grid(forward_rows_first(s, v1))
     a, kept = products(s, 0, ints, [u0, u2], x_fore, z_fore)
+    (f,) = products(s, 2, ints, [u1, u2, *kept], x_fore, z_fore)
     b, c = products(s, 1, ints, [u0, u1, u2], x_fore, z_fore)
-    (f,) = products(s, 2, ints, [u1, u2, *kept], x_fore, z_fore)
-    a, b, c, f = [backward_field(s, q) for q in (a, b, c, f)]
-    totals = lax.psum(jnp.sum(sums, axis=(2, 3)), "col") / (s.full_y * s.full_z)
+    a = backward_cols_first(s, a)
+    f = backward_rows_first(s, f)
+    b = backward_cols_first(s, b)
+    c = backward_cols_first(s, c)
+    own = jnp.sum(sums, axis=(2, 3))
+    shares = col_exchange(s, [own] * s.cols)
+    totals = ((shares[0] + shares[1]) + (shares[2] + shares[3])) / (s.full_y * s.full_z)
     spectra = jnp.stack([totals[:, 0], 2.0 * viscosity[0] * totals[:, 1]])
-    new_velocity, new_accumulator = tail(
-        s, ints, floats, velocity, accumulator, (a, b, c, f), y_fore
-    )
-    return new_velocity, new_accumulator, spectra
+    state = update(s, early_kernel, ints, floats, velocity, accumulator, (a, b), y_fore, {})
+    state = update(s, late_kernel, ints, floats, *state, (c, f), y_fore, {2: 0, 3: 1})
+    return (*state, spectra)
 
 
 def solution(mesh):

time: 438 us -> 460 us (1.050)
  blocking collectives: 77.8 us -> 31.9 us
  waiting for transfers between devices: 154 us -> 186 us
  Pallas kernels: 86.8 us -> 109 us
  starting transfers between devices: 83.7 us -> 99.7 us
    ppermute x21 -> x24, waiting for transfers between devices: 130 us -> 186 us  [col_exchange(): lax.ppermute(pieces[q], 'col', [(i, i ^ q) for i in range(s.cols)])]
    all_to_all x2 -> x1, blocking collectives: 61.7 us -> 31.9 us  [row_exchange(): return lax.all_to_all(field, 'row', 0, 0, tiled=True)]
    pallas_call x1 -> x6, Pallas kernels: 21.8 us -> 47.5 us  [the longest x2 36.4 us: update(): pl.pallas_call(functools.partial(kernel, s), grid=(s.width_x,), in_specs=...]
    all_to_all x5 -> x6, waiting for transfers between devices: 23.9 us -> 0.02 us  [row_exchange(): return lax.all_to_all(field, 'row', 0, 0, tiled=True)]
    psum x1 -> x0, blocking collectives: 16 us -> none  [tiled_body(): totals = lax.psum(jnp.sum(sums, axis=(2, 3)), 'col') / (s.full_y * s.full_z)]
    ppermute x21 -> x24, starting transfers between devices: 63.4 us -> 75.4 us  [col_exchange(): lax.ppermute(pieces[q], 'col', [(i, i ^ q) for i in range(s.cols)])]
    unnamed x30 -> x58, local copies, waits for them, and re-layouts: 5.77 us -> 10.9 us
    all_to_all x5 -> x6, starting transfers between devices: 20.3 us -> 24.4 us  [row_exchange(): return lax.all_to_all(field, 'row', 0, 0, tiled=True)]
  transfers between devices with their start and end apart: 26 -> 30, of which waited for: 12 -> 13; matrix products, arithmetic and copies ran while one was open for 4% -> 3% of each run, Pallas kernels for 8% -> 11%
where the time goes in v1:
time: 460 us; the launch traced here: 458 us
  waiting for transfers between devices  186 us (40%)
  Pallas kernels  109 us (24%)
  starting transfers between devices  99.7 us (22%)
  blocking collectives  31.9 us (7%)
  local copies, waits for them, and re-layouts  21.9 us (5%)
  other arithmetic  5.87 us (1%)
    ppermute x24, waiting for transfers between devices, col_exchange(): lax.ppermute(pieces[q], 'col', [(i, i ^ q) for i in range(s.cols)])  186 us
    ppermute x24, starting transfers between devices, col_exchange(): lax.ppermute(pieces[q], 'col', [(i, i ^ q) for i in range(s.cols)])  75.4 us
    pallas_call x2, Pallas kernels, update(): pl.pallas_call(functools.partial(kernel, s), grid=(s.width_x,), in_specs=...  36.4 us
    all_to_all x1, blocking collectives, row_exchange(): return lax.all_to_all(field, 'row', 0, 0, tiled=True)  31.9 us
    pallas_call x3, Pallas kernels, products(): pl.pallas_call(functools.partial(back_kernel, s, which), in_specs=[pl.Blo...  28.6 us
    all_to_all x6, starting transfers between devices, row_exchange(): return lax.all_to_all(field, 'row', 0, 0, tiled=True)  24.4 us
    pallas_call x3, Pallas kernels, to_grid(): pl.pallas_call(functools.partial(grid_kernel, s), in_specs=[pl.BlockSpec(...  20.4 us
    pallas_call x1, Pallas kernels, head(): pl.pallas_call(functools.partial(head_kernel, s), grid=(s.width_x // 2,),...  12.4 us
  transfers between devices with their start and end apart: 30, of which 13 were waited for; matrix products, arithmetic and copies ran while one was open for 3% of the time, Pallas kernels for 11%

profile of v1, /device:TPU:0, one launch (start us, length us, event | category | flops | bytes accessed | tf_op | source)
XLA Modules:
  0.0 458.3 jit_solution(15021025248208038147)
XLA Ops:
  5.1 12.4 %head.1 = (f32[8,4,16,8,128]{4,3,2,1,0:T(8,128)}, f32[8,4,16,8,128]{4,3,2,1,0:T(8,128)}, f32[8,16,8,128]{3,2,1,0:T(8,128)}, f32[8,16,8,128]{3,2,1,0:T(8,128)}, f...) custom-call(s32[18]{0:T(128)} %pad_add_fusion.ints, f32[4]{0:T(128)} %pad_maximum_fusion.3.floats, ...), custom_call_target="tpu_custom_call" | custom-call | tf_op jit(solution)/shard_map/head/pallas_call | solution.py:433
  17.5 31.9 %all_to_all.35 = f32[8,4,16,8,128]{4,3,2,1,0:T(8,128)} all-to-all(f32[8,4,16,8,128]{4,3,2,1,0:T(8,128)} %get-tuple-element.34), channel_id=1, replica_groups=mesh['row'=8,'col'=4] {'row'}, dimensions={0} | all-to-all | bytes 4194304 | tf_op jit(solution)/shard_map/all_to_all | solution.py:680
  57.9 20.8 %collective-permute-done.3 = f32[8,16,8,128]{3,2,1,0:T(8,128)S(1)} collective-permute-done((f32[8,16,8,128]{3,2,1,0:T(8,128)}, f32[8,16,8,128]{3,2,1,0:T(8,128)S(1)}, u32[]{:S(2)}, u32[]{:S(2)}) %collective-permute-start.3) | collective-permute-done | bytes 524320 | tf_op jit(solution)/shard_map/ppermute | solution.py:675
  78.7 15.1 %collective-permute-done.4 = f32[8,16,8,128]{3,2,1,0:T(8,128)S(1)} collective-permute-done((f32[8,16,8,128]{3,2,1,0:T(8,128)}, f32[8,16,8,128]{3,2,1,0:T(8,128)S(1)}, u32[]{:S(2)}, u32[]{:S(2)}) %collective-permute-start.4) | collective-permute-done | bytes 524320 | tf_op jit(solution)/shard_map/ppermute | solution.py:675
  102.5 10.8 %collective-permute-start = (f32[88,8,128]{2,1,0:T(8,128)S(1)}, f32[88,8,128]{2,1,0:T(8,128)S(1)}, u32[]{:S(2)}, u32[]{:S(2)}) collective-permute-start(f32[88,8,128]{2,1,0:T(8,128)S(1)} %slice.123), channel_id=1, source_target_pairs={{0,1},{1,0},{2,3},{3,2},{4,5},{5,4},{6,7},{7,6},{8,9},{9,8},{10,11... | collective-permute-start | bytes 1081352 | tf_op jit(solution)/shard_map/ppermute | solution.py:675
  120.6 9.0 %collective-permute-done.refs_1_ = f32[88,8,128]{2,1,0:T(8,128)S(1)} collective-permute-done((f32[88,8,128]{2,1,0:T(8,128)S(1)}, f32[88,8,128]{2,1,0:T(8,128)S(1)}, u32[]{:S(2)}, u32[]{:S(2)}) %collective-permute-start) | collective-permute-done | bytes 360480 | tf_op jit(solution)/shard_map/ppermute | solution.py:675
  132.6 8.8 %collective-permute-done.1.refs_2_ = f32[88,8,128]{2,1,0:T(8,128)S(1)} collective-permute-done((f32[88,8,128]{2,1,0:T(8,128)S(1)}, f32[88,8,128]{2,1,0:T(8,128)S(1)}, u32[]{:S(2)}, u32[]{:S(2)}) %collective-permute-start.1) | collective-permute-done | bytes 360480 | tf_op jit(solution)/shard_map/ppermute | solution.py:675
  149.7 22.6 %collective-permute-done.10.refs_2_ = f32[88,8,128]{2,1,0:T(8,128)S(1)} collective-permute-done((f32[88,8,128]{2,1,0:T(8,128)S(1)}, f32[88,8,128]{2,1,0:T(8,128)S(1)}, u32[]{:S(2)}, u32[]{:S(2)}) %collective-permute-start.10) | collective-permute-done | bytes 360480 | tf_op jit(solution)/shard_map/ppermute | solution.py:675
  190.7 10.2 %shard_map.184 = (f32[88,8,128]{2,1,0:T(8,128)}, f32[88,8,128]{2,1,0:T(8,128)}, f32[88,8,128]{2,1,0:T(8,128)}, f32[88,8,128]{2,1,0:T(8,128)}, f32[88,8,128]{2,1,...) custom-call(s32[18]{0:T(128)} %pad_add_fusion.ints, ...), custom_call_target="tpu_custom_call" | custom-call | tf_op jit(solution)/shard_map/pallas_call | solution.py:574
  201.0 7.7 %shard_map.187 = (f32[88,8,128]{2,1,0:T(8,128)}, f32[88,8,128]{2,1,0:T(8,128)}, f32[88,8,128]{2,1,0:T(8,128)}, f32[88,8,128]{2,1,0:T(8,128)}) custom-call(s32[18]{0:T(128)} %pad_add_fusion.ints, f32[8,256,256]{2,1,0:T(8,128)} %to_grid.5.refs_1_.refs_0_, f32[8,256,256]{2,1,0:T(8,128)} %to_grid.4.refs_1_.refs_2_, f32[88,8,128]{2,1,0:T(8,128)} %get-tuple-element.54.refs_2_, ...), custom_call_target="tpu_custom_call" | custom-call | tf_op jit(solution)/shard_map/pallas_call | solution.py:574
  215.6 10.6 %shard_map.185 = (f32[88,8,128]{2,1,0:T(8,128)}, f32[88,8,128]{2,1,0:T(8,128)}, f32[88,8,128]{2,1,0:T(8,128)}, f32[88,8,128]{2,1,0:T(8,128)}, f32[88,8,128]{2,1,...) custom-call(s32[18]{0:T(128)} %pad_add_fusion.ints, ...), custom_call_target="tpu_custom_call" | custom-call | tf_op jit(solution)/shard_map/pallas_call | solution.py:574
  235.2 14.1 %collective-permute-done.12.refs_1_ = f32[88,8,128]{2,1,0:T(8,128)S(1)} collective-permute-done((f32[88,8,128]{2,1,0:T(8,128)}, f32[88,8,128]{2,1,0:T(8,128)S(1)}, u32[]{:S(2)}, u32[]{:S(2)}) %collective-permute-start.12) | collective-permute-done | bytes 360480 | tf_op jit(solution)/shard_map/ppermute | solution.py:675
  249.4 11.3 %collective-permute-done.13.refs_2_ = f32[88,8,128]{2,1,0:T(8,128)S(1)} collective-permute-done((f32[88,8,128]{2,1,0:T(8,128)}, f32[88,8,128]{2,1,0:T(8,128)S(1)}, u32[]{:S(2)}, u32[]{:S(2)}) %collective-permute-start.13) | collective-permute-done | bytes 360480 | tf_op jit(solution)/shard_map/ppermute | solution.py:675
  269.8 7.1 %collective-permute-start.6 = (f32[88,8,128]{2,1,0:T(8,128)S(1)}, f32[88,8,128]{2,1,0:T(8,128)S(1)}, u32[]{:S(2)}, u32[]{:S(2)}) collective-permute-start(f32[88,8,128]{2,1,0:T(8,128)S(1)} %copy-done.28), channel_id=1, source_target_pairs={{0,1},{1,0},{2,3},{3,2},{4,5},{5,4},{6,7},{7,6},{8,9},{9,8},{10,11... | collective-permute-start | bytes 1081352 | tf_op jit(solution)/shard_map/ppermute | solution.py:675
  279.4 13.8 %collective-permute-done.6.refs_1_ = f32[88,8,128]{2,1,0:T(8,128)S(1)} collective-permute-done((f32[88,8,128]{2,1,0:T(8,128)S(1)}, f32[88,8,128]{2,1,0:T(8,128)S(1)}, u32[]{:S(2)}, u32[]{:S(2)}) %collective-permute-start.6) | collective-permute-done | bytes 360480 | tf_op jit(solution)/shard_map/ppermute | solution.py:675
  293.2 11.4 %collective-permute-done.7.refs_2_ = f32[88,8,128]{2,1,0:T(8,128)S(1)} collective-permute-done((f32[88,8,128]{2,1,0:T(8,128)S(1)}, f32[88,8,128]{2,1,0:T(8,128)S(1)}, u32[]{:S(2)}, u32[]{:S(2)}) %collective-permute-start.7) | collective-permute-done | bytes 360480 | tf_op jit(solution)/shard_map/ppermute | solution.py:675
  313.9 7.4 %collective-permute-start.15 = (f32[88,8,128]{2,1,0:T(8,128)S(1)}, f32[88,8,128]{2,1,0:T(8,128)S(1)}, u32[]{:S(2)}, u32[]{:S(2)}) collective-permute-start(f32[88,8,128]{2,1,0:T(8,128)S(1)} %copy-done.25), channel_id=1, source_target_pairs={{0,1},{1,0},{2,3},{3,2},{4,5},{5,4},{6,7},{7,6},{8,9},{9,8},{10,11... | collective-permute-start | bytes 1081352 | tf_op jit(solution)/shard_map/ppermute | solution.py:675
  323.8 13.6 %collective-permute-done.15.refs_1_ = f32[88,8,128]{2,1,0:T(8,128)S(1)} collective-permute-done((f32[88,8,128]{2,1,0:T(8,128)S(1)}, f32[88,8,128]{2,1,0:T(8,128)S(1)}, u32[]{:S(2)}, u32[]{:S(2)}) %collective-permute-start.15) | collective-permute-done | bytes 360480 | tf_op jit(solution)/shard_map/ppermute | solution.py:675
  337.4 11.6 %collective-permute-done.16.refs_2_ = f32[88,8,128]{2,1,0:T(8,128)S(1)} collective-permute-done((f32[88,8,128]{2,1,0:T(8,128)S(1)}, f32[88,8,128]{2,1,0:T(8,128)S(1)}, u32[]{:S(2)}, u32[]{:S(2)}) %collective-permute-start.16) | collective-permute-done | bytes 360480 | tf_op jit(solution)/shard_map/ppermute | solution.py:675
  359.4 8.0 %collective-permute-start.19 = (f32[8,16,8,128]{3,2,1,0:T(8,128)}, f32[8,16,8,128]{3,2,1,0:T(8,128)}, u32[]{:S(2)}, u32[]{:S(2)}) collective-permute-start(f32[8,16,8,128]{3,2,1,0:T(8,128)} %get-tuple-element.68), channel_id=1, source_target_pairs={{0,2},{1,3},{2,0},{3,1},{4,6},{5,7},{6,4},{7,5},{8,10},{9,11},{10,... | collective-permute-start | bytes 1572872 | tf_op jit(solution)/shard_map/ppermute | solution.py:675
  371.6 32.6 %collective-permute-done.23 = f32[16,2]{1,0:T(8,128)S(1)} collective-permute-done((f32[16,2]{1,0:T(8,128)S(1)}, f32[16,2]{1,0:T(8,128)S(1)}, u32[]{:S(2)}, u32[]{:S(2)}) %collective-permute-start.23) | collective-permute-done | bytes 160 | tf_op jit(solution)/shard_map/ppermute | solution.py:675
  404.3 10.9 %collective-permute-start.21 = (f32[16,2]{1,0:T(8,128)S(1)}, f32[16,2]{1,0:T(8,128)S(1)}, u32[]{:S(2)}, u32[]{:S(2)}) collective-permute-start(f32[16,2]{1,0:T(8,128)S(1)} %reduce_sum.9), channel_id=1, source_target_pairs={{0,1},{1,0},{2,3},{3,2},{4,5},{5,4},{6,7},{7,6},{8,9},{9,8},{10,11... | collective-permute-start | bytes 392 | tf_op jit(solution)/shard_map/ppermute | solution.py:675
  417.6 18.6 %shard_map.186 = (f32[3,2,16,64,256]{4,3,2,1,0:T(8,128)}, f32[3,2,16,64,256]{4,3,2,1,0:T(8,128)}) custom-call(s32[18]{0:T(128)} %pad_add_fusion.ints, f32[4]{0:T(128)} %pad_maximum_fusion.3.floats, f32[3,2,16,64,256]{4,3,2,1,0:T(8,128)} %vel.3, f32[3,2,16,64,256]{4,3,2,1,0:T(8,128)} %acc.1, f32[8,4,16,8,128]{4,3,2,1,0:T(8,128)} %all-to-all-done.2.fa, ...), custom_call_target="tpu_custom_call" | custom-call | tf_op jit(solution)/shard_map/pallas_call | solution.py:658
  440.5 17.8 %shard_map.188 = (f32[3,2,16,64,256]{4,3,2,1,0:T(8,128)}, f32[3,2,16,64,256]{4,3,2,1,0:T(8,128)}) custom-call(s32[18]{0:T(128)} %pad_add_fusion.ints, f32[4]{0:T(128)} %pad_maximum_fusion.3.floats, f32[3,2,16,64,256]{4,3,2,1,0:T(8,128)} %get-tuple-element.48.vel, ...), custom_call_target="tpu_custom_call", output_to_operand_aliasing={{0}: (2, {}), {1}: (3, {})} | custom-call | tf_op jit(solution)/shard_map/pallas_call | solution.py:658
  (134 shorter events, 116.5 us)
Async XLA Ops:
  49.4 46.1 %all-to-all-start.3 = ((f32[8,4,16,8,128]{4,3,2,1,0:T(8,128)}), f32[8,4,16,8,128]{4,3,2,1,0:T(8,128)S(1)}, u32[]{:S(2)}, u32[]{:S(2)}) async-start(f32[8,4,16,8,128]{4,3,2,1,0:T(8,128)} %get-tuple-element.43), calls=%async_computation.3 | async-start | bytes 4194304 | tf_op jit(solution)/shard_map/all_to_all | solution.py:680
  55.3 38.4 %collective-permute-start.4 = (f32[8,16,8,128]{3,2,1,0:T(8,128)}, f32[8,16,8,128]{3,2,1,0:T(8,128)S(1)}, u32[]{:S(2)}, u32[]{:S(2)}) collective-permute-start(f32[8,16,8,128]{3,2,1,0:T(8,128)} %get-tuple-element.37), channel_id=1, source_target_pairs={{0,2},{1,3},{2,0},{3,1},{4,6},{5,7},{6,4},{7,5},{8,10},{9,11},{10,... | collective-permute-start | bytes 1572872 | tf_op jit(solution)/shard_map/ppermute | solution.py:675
  57.9 35.8 %collective-permute-start.5 = (f32[8,16,8,128]{3,2,1,0:T(8,128)S(1)}, f32[8,16,8,128]{3,2,1,0:T(8,128)S(1)}, u32[]{:S(2)}, u32[]{:S(2)}) collective-permute-start(f32[8,16,8,128]{3,2,1,0:T(8,128)S(1)} %copy-done.22), channel_id=1, source_target_pairs={{0,3},{1,2},{2,1},{3,0},{4,7},{5,6},{6,5},{7,4},{8,11},{9,10},{10,... | collective-permute-start | bytes 1572872 | tf_op jit(solution)/shard_map/ppermute | solution.py:675
  96.8 83.9 %all-to-all-start.1 = ((f32[8,4,16,8,128]{4,3,2,1,0:T(8,128)}), f32[8,4,16,8,128]{4,3,2,1,0:T(8,128)S(1)}, u32[]{:S(2)}, u32[]{:S(2)}) async-start(f32[8,4,16,8,128]{4,3,2,1,0:T(8,128)} %copy.30), calls=%async_computation.1 | async-start | bytes 4194304 | tf_op jit(solution)/shard_map/all_to_all | solution.py:680
  102.5 27.1 %collective-permute-start = (f32[88,8,128]{2,1,0:T(8,128)S(1)}, f32[88,8,128]{2,1,0:T(8,128)S(1)}, u32[]{:S(2)}, u32[]{:S(2)}) collective-permute-start(f32[88,8,128]{2,1,0:T(8,128)S(1)} %slice.123), channel_id=1, source_target_pairs={{0,1},{1,0},{2,3},{3,2},{4,5},{5,4},{6,7},{7,6},{8,9},{9,8},{10,11... | collective-permute-start | bytes 1081352 | tf_op jit(solution)/shard_map/ppermute | solution.py:675
  113.7 27.8 %collective-permute-start.1 = (f32[88,8,128]{2,1,0:T(8,128)S(1)}, f32[88,8,128]{2,1,0:T(8,128)S(1)}, u32[]{:S(2)}, u32[]{:S(2)}) collective-permute-start(f32[88,8,128]{2,1,0:T(8,128)S(1)} %slice.125), channel_id=1, source_target_pairs={{0,2},{1,3},{2,0},{3,1},{4,6},{5,7},{6,4},{7,5},{8,10},{9,11},{10,... | collective-permute-start | bytes 1081352 | tf_op jit(solution)/shard_map/ppermute | solution.py:675
  117.5 32.2 %collective-permute-start.9 = (f32[88,8,128]{2,1,0:T(8,128)S(1)}, f32[88,8,128]{2,1,0:T(8,128)S(1)}, u32[]{:S(2)}, u32[]{:S(2)}) collective-permute-start(f32[88,8,128]{2,1,0:T(8,128)S(1)} %slice.139), channel_id=1, source_target_pairs={{0,1},{1,0},{2,3},{3,2},{4,5},{5,4},{6,7},{7,6},{8,9},{9,8},{10,11... | collective-permute-start | bytes 1081352 | tf_op jit(solution)/shard_map/ppermute | solution.py:675
  117.6 54.7 %collective-permute-start.10 = (f32[88,8,128]{2,1,0:T(8,128)S(1)}, f32[88,8,128]{2,1,0:T(8,128)S(1)}, u32[]{:S(2)}, u32[]{:S(2)}) collective-permute-start(f32[88,8,128]{2,1,0:T(8,128)S(1)} %slice.141), channel_id=1, source_target_pairs={{0,2},{1,3},{2,0},{3,1},{4,6},{5,7},{6,4},{7,5},{8,10},{9,11},{10,... | collective-permute-start | bytes 1081352 | tf_op jit(solution)/shard_map/ppermute | solution.py:675
  129.6 42.7 %collective-permute-start.11 = (f32[88,8,128]{2,1,0:T(8,128)S(1)}, f32[88,8,128]{2,1,0:T(8,128)S(1)}, u32[]{:S(2)}, u32[]{:S(2)}) collective-permute-start(f32[88,8,128]{2,1,0:T(8,128)S(1)} %slice.143), channel_id=1, source_target_pairs={{0,3},{1,2},{2,1},{3,0},{4,7},{5,6},{6,5},{7,4},{8,11},{9,10},{10,... | collective-permute-start | bytes 1081352 | tf_op jit(solution)/shard_map/ppermute | solution.py:675
  211.5 52.9 %all-to-all-start.6 = ((f32[8,4,16,8,128]{4,3,2,1,0:T(8,128)}), f32[8,4,16,8,128]{4,3,2,1,0:T(8,128)S(1)}, u32[]{:S(2)}, u32[]{:S(2)}) async-start(f32[8,4,16,8,128]{4,3,2,1,0:T(8,128)} %spread.7), calls=%async_computation.6 | async-start | bytes 4194304 | tf_op jit(solution)/shard_map/all_to_all | solution.py:680
  232.8 27.9 %collective-permute-start.13 = (f32[88,8,128]{2,1,0:T(8,128)}, f32[88,8,128]{2,1,0:T(8,128)S(1)}, u32[]{:S(2)}, u32[]{:S(2)}) collective-permute-start(f32[88,8,128]{2,1,0:T(8,128)} %get-tuple-element.46), channel_id=1, source_target_pairs={{0,2},{1,3},{2,0},{3,1},{4,6},{5,7},{6,4},{7,5},{8,10},{9,11},{10,... | collective-permute-start | bytes 1081352 | tf_op jit(solution)/shard_map/ppermute | solution.py:675
  233.8 26.9 %collective-permute-start.14 = (f32[88,8,128]{2,1,0:T(8,128)}, f32[88,8,128]{2,1,0:T(8,128)S(1)}, u32[]{:S(2)}, u32[]{:S(2)}) collective-permute-start(f32[88,8,128]{2,1,0:T(8,128)} %get-tuple-element.47), channel_id=1, source_target_pairs={{0,3},{1,2},{2,1},{3,0},{4,7},{5,6},{6,5},{7,4},{8,11},{9,10},{10,... | collective-permute-start | bytes 1081352 | tf_op jit(solution)/shard_map/ppermute | solution.py:675
  265.7 42.6 %all-to-all-start.4 = ((f32[8,4,16,8,128]{4,3,2,1,0:T(8,128)}), f32[8,4,16,8,128]{4,3,2,1,0:T(8,128)S(1)}, u32[]{:S(2)}, u32[]{:S(2)}) async-start(f32[8,4,16,8,128]{4,3,2,1,0:T(8,128)} %spread.5), calls=%async_computation.4 | async-start | bytes 4194304 | tf_op jit(solution)/shard_map/all_to_all | solution.py:680
  276.9 27.7 %collective-permute-start.7 = (f32[88,8,128]{2,1,0:T(8,128)S(1)}, f32[88,8,128]{2,1,0:T(8,128)S(1)}, u32[]{:S(2)}, u32[]{:S(2)}) collective-permute-start(f32[88,8,128]{2,1,0:T(8,128)S(1)} %copy-done.27), channel_id=1, source_target_pairs={{0,2},{1,3},{2,0},{3,1},{4,6},{5,7},{6,4},{7,5},{8,10},{9,11},{10,... | collective-permute-start | bytes 1081352 | tf_op jit(solution)/shard_map/ppermute | solution.py:675
  278.0 26.7 %collective-permute-start.8 = (f32[88,8,128]{2,1,0:T(8,128)S(1)}, f32[88,8,128]{2,1,0:T(8,128)S(1)}, u32[]{:S(2)}, u32[]{:S(2)}) collective-permute-start(f32[88,8,128]{2,1,0:T(8,128)S(1)} %copy-done.26), channel_id=1, source_target_pairs={{0,3},{1,2},{2,1},{3,0},{4,7},{5,6},{6,5},{7,4},{8,11},{9,10},{10,... | collective-permute-start | bytes 1081352 | tf_op jit(solution)/shard_map/ppermute | solution.py:675
  309.6 43.1 %all-to-all-start.2 = ((f32[8,4,16,8,128]{4,3,2,1,0:T(8,128)}), f32[8,4,16,8,128]{4,3,2,1,0:T(8,128)}, u32[]{:S(2)}, u32[]{:S(2)}) async-start(f32[8,4,16,8,128]{4,3,2,1,0:T(8,128)} %spread.4), calls=%async_computation.2 | async-start | bytes 4194304 | tf_op jit(solution)/shard_map/all_to_all | solution.py:680
  321.3 27.7 %collective-permute-start.16 = (f32[88,8,128]{2,1,0:T(8,128)S(1)}, f32[88,8,128]{2,1,0:T(8,128)S(1)}, u32[]{:S(2)}, u32[]{:S(2)}) collective-permute-start(f32[88,8,128]{2,1,0:T(8,128)S(1)} %copy-done.24), channel_id=1, source_target_pairs={{0,2},{1,3},{2,0},{3,1},{4,6},{5,7},{6,4},{7,5},{8,10},{9,11},{10,... | collective-permute-start | bytes 1081352 | tf_op jit(solution)/shard_map/ppermute | solution.py:675
  322.4 26.7 %collective-permute-start.17 = (f32[88,8,128]{2,1,0:T(8,128)S(1)}, f32[88,8,128]{2,1,0:T(8,128)S(1)}, u32[]{:S(2)}, u32[]{:S(2)}) collective-permute-start(f32[88,8,128]{2,1,0:T(8,128)S(1)} %copy-done.23), channel_id=1, source_target_pairs={{0,3},{1,2},{2,1},{3,0},{4,7},{5,6},{6,5},{7,4},{8,11},{9,10},{10,... | collective-permute-start | bytes 1081352 | tf_op jit(solution)/shard_map/ppermute | solution.py:675
  352.7 86.4 %all-to-all-start.5 = ((f32[8,4,16,8,128]{4,3,2,1,0:T(8,128)}), f32[8,4,16,8,128]{4,3,2,1,0:T(8,128)S(1)}, u32[]{:S(2)}, u32[]{:S(2)}) async-start(f32[8,4,16,8,128]{4,3,2,1,0:T(8,128)} %spread.6), calls=%async_computation.5 | async-start | bytes 4194304 | tf_op jit(solution)/shard_map/all_to_all | solution.py:680
  359.4 76.8 %collective-permute-start.19 = (f32[8,16,8,128]{3,2,1,0:T(8,128)}, f32[8,16,8,128]{3,2,1,0:T(8,128)}, u32[]{:S(2)}, u32[]{:S(2)}) collective-permute-start(f32[8,16,8,128]{3,2,1,0:T(8,128)} %get-tuple-element.68), channel_id=1, source_target_pairs={{0,2},{1,3},{2,0},{3,1},{4,6},{5,7},{6,4},{7,5},{8,10},{9,11},{10,... | collective-permute-start | bytes 1572872 | tf_op jit(solution)/shard_map/ppermute | solution.py:675
  367.4 68.8 %collective-permute-start.18 = (f32[8,16,8,128]{3,2,1,0:T(8,128)}, f32[8,16,8,128]{3,2,1,0:T(8,128)}, u32[]{:S(2)}, u32[]{:S(2)}) collective-permute-start(f32[8,16,8,128]{3,2,1,0:T(8,128)} %get-tuple-element.69), channel_id=1, source_target_pairs={{0,1},{1,0},{2,3},{3,2},{4,5},{5,4},{6,7},{7,6},{8,9},{9,8},{10,11... | collective-permute-start | bytes 1572872 | tf_op jit(solution)/shard_map/ppermute | solution.py:675
  367.4 68.8 %collective-permute-start.20 = (f32[8,16,8,128]{3,2,1,0:T(8,128)S(1)}, f32[8,16,8,128]{3,2,1,0:T(8,128)}, u32[]{:S(2)}, u32[]{:S(2)}) collective-permute-start(f32[8,16,8,128]{3,2,1,0:T(8,128)S(1)} %get-tuple-element.70), channel_id=1, source_target_pairs={{0,3},{1,2},{2,1},{3,0},{4,7},{5,6},{6,5},{7,4},{8,11},{9,10},{10,... | collective-permute-start | bytes 1572872 | tf_op jit(solution)/shard_map/ppermute | solution.py:675
  369.0 35.2 %collective-permute-start.23 = (f32[16,2]{1,0:T(8,128)S(1)}, f32[16,2]{1,0:T(8,128)S(1)}, u32[]{:S(2)}, u32[]{:S(2)}) collective-permute-start(f32[16,2]{1,0:T(8,128)S(1)} %reduce_sum.9), channel_id=1, source_target_pairs={{0,3},{1,2},{2,1},{3,0},{4,7},{5,6},{6,5},{7,4},{8,11},{9,10},{10,... | collective-permute-start | bytes 392 | tf_op jit(solution)/shard_map/ppermute | solution.py:675
  371.5 43.7 %collective-permute-start.22 = (f32[16,2]{1,0:T(8,128)S(1)}, f32[16,2]{1,0:T(8,128)S(1)}, u32[]{:S(2)}, u32[]{:S(2)}) collective-permute-start(f32[16,2]{1,0:T(8,128)S(1)} %reduce_sum.9), channel_id=1, source_target_pairs={{0,2},{1,3},{2,0},{3,1},{4,6},{5,7},{6,4},{7,5},{8,10},{9,11},{10,... | collective-permute-start | bytes 392 | tf_op jit(solution)/shard_map/ppermute | solution.py:675
  (35 other events, 355.7 us)

commit v2 on v1

--- a/solution.py
+++ b/solution.py
@@ -12,6 +12,7 @@
 
 F32 = jnp.float32
 BF16 = jnp.bfloat16
+ROWS_A_STEP = 8
 VMEM_LIMIT = 56 * 1024 * 1024
 
 
@@ -329,7 +330,7 @@
             and self.full_y % 128 == 0
             and self.full_z % 128 == 0
             and self.full_x % 128 == 0
-            and self.width_x % 2 == 0
+            and self.width_x % ROWS_A_STEP == 0
             and self.rows & (self.rows - 1) == 0
             and self.cols & (self.cols - 1) == 0
         )
@@ -423,10 +424,7 @@
                 at = pl.multiple_of((r * s.cols + (q ^ col)) * 8, 8)
                 for j in range(2):
                     tile = made[pl.ds(at, 8), j * 128 : (j + 1) * 128]
-                    if c < 2:
-                        fields[c][r, q, j] = tile
-                    else:
-                        fields[c + q][r, j] = tile
+                    fields[c][r, q, j] = tile
 
 
 def head(s, ints, floats, velocity, table):
@@ -439,17 +437,15 @@
             pl.BlockSpec((3, 2, 2, s.width_z, s.full_y), lambda i: (0, 0, i, 0, 0)),
             whole(table.shape),
         ],
-        out_specs=[pl.BlockSpec((s.rows, s.cols, 2, 8, s.lanes), lambda i: (0, 0, i, 0, 0))] * 2
-        + [pl.BlockSpec((s.rows, 2, 8, s.lanes), lambda i: (0, i, 0, 0))] * s.cols
+        out_specs=[pl.BlockSpec((s.rows, s.cols, 2, 8, s.lanes), lambda i: (0, 0, i, 0, 0))] * 3
         + [pl.BlockSpec((2, 2, 8, s.full_y), lambda i: (i, 0, 0, 0))],
-        out_shape=[jax.ShapeDtypeStruct((s.rows, s.cols, s.width_x, 8, s.lanes), F32)] * 2
-        + [jax.ShapeDtypeStruct((s.rows, s.width_x, 8, s.lanes), F32)] * s.cols
+        out_shape=[jax.ShapeDtypeStruct((s.rows, s.cols, s.width_x, 8, s.lanes), F32)] * 3
         + [jax.ShapeDtypeStruct((s.width_x, 2, 8, s.full_y), F32)],
         scratch_shapes=[pltpu.VMEM((s.full_y, 256), F32)],
         compiler_params=pltpu.CompilerParams(vmem_limit_bytes=VMEM_LIMIT),
         name="head",
     )(ints, floats, velocity, table)
-    return out[0], out[1], out[2:-1], out[-1]
+    return out
 
 
 def grid_kernel(s, ints, *refs):
@@ -591,10 +587,10 @@
     return (k0, k1, k2), ksq, inverse, mask, flat, flat * scale, cosine, sine
 
 
-def modes_of(s, col, refs, yh, yl):
+def modes_of(s, j, col, refs, yh, yl):
     turned = []
     for ref in refs:
-        tiles = [ref[r, q ^ col, 0] for r in range(s.rows) for q in range(s.cols)]
+        tiles = [ref[r, q ^ col, j] for r in range(s.rows) for q in range(s.cols)]
         turned.append(jnp.concatenate(tiles, axis=0).T)
     every = by_right_table(jnp.concatenate(turned, axis=0), yh[...], yl[...])
     modes = []
@@ -605,14 +601,14 @@
     return modes
 
 
-def early_kernel(s, ints, floats, vel, acc, fa, fb, yh, yl, new_vel, new_acc):
+def early_row(s, j, ints, floats, vel, acc, fa, fb, yh, yl, new_vel, new_acc):
     row, col = ints[0], ints[1]
-    local = pl.program_id(0)
+    local = ROWS_A_STEP * pl.program_id(0) + j
     kx, amount = row * s.width_x + local, ints[2 + local]
-    modes = modes_of(s, col, (fa, fb), yh, yl)
+    modes = modes_of(s, j, col, (fa, fb), yh, yl)
     k, ksq, inverse, mask, _, kh, cosine, sine = frame(s, kx, col, floats[0])
-    v = rolled(s, vel, 0, amount)
-    old = rolled(s, acc, 0, amount)
+    v = rolled(s, vel, j, amount)
+    old = rolled(s, acc, j, amount)
     shear, viscosity, dt = floats[1], floats[2], floats[3]
     coupling = (2.0 * shear) * k[0] * inverse
     for p in range(2):
@@ -627,14 +623,14 @@
             if c3 == 0:
                 rate = rate - shear * v[1][p]
             fresh = (-5.0 / 9.0) * old[c3][p] + dt * rate
-            new_acc[c3, p, 0] = fresh
-            new_vel[c3, p, 0] = v[c3][p] + (15.0 / 16.0) * fresh
-
-
-def late_kernel(s, ints, floats, vel, acc, fc, ff, yh, yl, new_vel, new_acc):
+            new_acc[c3, p, j] = fresh
+            new_vel[c3, p, j] = v[c3][p] + (15.0 / 16.0) * fresh
+
+
+def late_row(s, j, ints, floats, vel, acc, fc, ff, yh, yl, new_vel, new_acc):
     row, col = ints[0], ints[1]
-    kx = row * s.width_x + pl.program_id(0)
-    modes = modes_of(s, col, (fc, ff), yh, yl)
+    kx = row * s.width_x + ROWS_A_STEP * pl.program_id(0) + j
+    modes = modes_of(s, j, col, (fc, ff), yh, yl)
     k, _, inverse, mask, flat, kh, cosine, sine = frame(s, kx, col, floats[0])
     dt = floats[3] * mask
     lean = dt * (flat - k[1] * k[1]) * inverse
@@ -646,18 +642,28 @@
             qe = -qe
         slope = qe * k[1]
         for c3, add in enumerate((-(slope * cosine), qe * kh, -(slope * sine))):
-            new_acc[c3, p, 0] = acc[c3, p, 0] + add
-            new_vel[c3, p, 0] = vel[c3, p, 0] + (15.0 / 16.0) * add
+            new_acc[c3, p, j] = acc[c3, p, j] + add
+            new_vel[c3, p, j] = vel[c3, p, j] + (15.0 / 16.0) * add
+
+
+def each_row(one, s, *refs):
+    for j in range(ROWS_A_STEP):
+        one(s, j, *refs)
+
+
+early_kernel = functools.partial(each_row, early_row)
+late_kernel = functools.partial(each_row, late_row)
 
 
 def update(s, kernel, ints, floats, velocity, accumulator, fields, table, alias):
-    plane = pl.BlockSpec((3, 2, 1, s.width_z, s.full_y), lambda i: (0, 0, i, 0, 0))
-    piece = pl.BlockSpec((s.rows, s.cols, 1, 8, s.lanes), lambda i: (0, 0, i, 0, 0))
+    n = ROWS_A_STEP
+    plane = pl.BlockSpec((3, 2, n, s.width_z, s.full_y), lambda i: (0, 0, i, 0, 0))
+    piece = pl.BlockSpec((s.rows, s.cols, n, 8, s.lanes), lambda i: (0, 0, i, 0, 0))
     y2 = (s.full_y, 2 * s.full_y)
     shape = jax.ShapeDtypeStruct(velocity.shape, F32)
     return pl.pallas_call(
         functools.partial(kernel, s),
-        grid=(s.width_x,),
+        grid=(s.width_x // n,),
         in_specs=[pl.BlockSpec(memory_space=pltpu.SMEM)] * 2
         + [plane] * 2
         + [piece] * 2
@@ -710,10 +716,6 @@
     return col_exchange(s, of_cols(s, row_exchange(field)))
 
 
-def forward_cols_first(s, pieces):
-    return of_cols(s, row_exchange(jnp.stack(col_exchange(s, pieces), axis=1)))
-
-
 def backward_cols_first(s, pieces):
     return row_exchange(of_rows(s, col_exchange(s, pieces)))
 
@@ -734,7 +736,7 @@
         return to_grid(s, ints, pieces, z_back, x_back)
 
     u0 = grid(forward_rows_first(s, v0))
-    u2 = grid(forward_cols_first(s, v2))
+    u2 = grid(forward_rows_first(s, v2))
     u1 = grid(forward_rows_first(s, v1))
     a, kept = products(s, 0, ints, [u0, u2], x_fore, z_fore)
     (f,) = products(s, 2, ints, [u1, u2, *kept], x_fore, z_fore)

time: 460 us -> 439 us (0.954)
  waiting for transfers between devices: 186 us -> 150 us
  blocking collectives: 31.9 us -> 61.7 us
  Pallas kernels: 109 us -> 96.3 us
    ppermute x24, waiting for transfers between devices: 186 us -> 136 us  [col_exchange(): lax.ppermute(pieces[q], 'col', [(i, i ^ q) for i in range(s.cols)])]
    all_to_all x1 -> x2, blocking collectives: 31.9 us -> 61.7 us  [row_exchange(): return lax.all_to_all(field, 'row', 0, 0, tiled=True)]
    all_to_all x6 -> x5, waiting for transfers between devices: 0.02 us -> 14.2 us  [row_exchange(): return lax.all_to_all(field, 'row', 0, 0, tiled=True)]
    pallas_call x2, Pallas kernels: 36.4 us -> 23.9 us  [update(): pl.pallas_call(functools.partial(kernel, s), grid=(s.width_x // n,), in_s...]
    all_to_all x6 -> x5, starting transfers between devices: 24.4 us -> 20.2 us  [row_exchange(): return lax.all_to_all(field, 'row', 0, 0, tiled=True)]
    unnamed x58 -> x54, local copies, waits for them, and re-layouts: 10.9 us -> 10.4 us
  transfers between devices with their start and end apart: 30 -> 29, of which waited for: 13 -> 10; matrix products, arithmetic and copies ran while one was open for 3% -> 3% of each run, Pallas kernels for 11% -> 13%
where the time goes in v2:
time: 439 us; the launch traced here: 438 us
  waiting for transfers between devices  150 us (34%)
  starting transfers between devices  99 us (23%)
  Pallas kernels  96.3 us (22%)
  blocking collectives  61.7 us (14%)
  local copies, waits for them, and re-layouts  21.5 us (5%)
  other arithmetic  5.79 us (1%)
    ppermute x24, waiting for transfers between devices, col_exchange(): lax.ppermute(pieces[q], 'col', [(i, i ^ q) for i in range(s.cols)])  136 us
    ppermute x24, starting transfers between devices, col_exchange(): lax.ppermute(pieces[q], 'col', [(i, i ^ q) for i in range(s.cols)])  78.8 us
    all_to_all x2, blocking collectives, row_exchange(): return lax.all_to_all(field, 'row', 0, 0, tiled=True)  61.7 us
    pallas_call x3, Pallas kernels, products(): pl.pallas_call(functools.partial(back_kernel, s, which), in_specs=[pl.Blo...  28.4 us
    pallas_call x2, Pallas kernels, update(): pl.pallas_call(functools.partial(kernel, s), grid=(s.width_x // n,), in_s...  23.9 us
    pallas_call x3, Pallas kernels, to_grid(): pl.pallas_call(functools.partial(grid_kernel, s), in_specs=[pl.BlockSpec(...  20.5 us
    all_to_all x5, starting transfers between devices, row_exchange(): return lax.all_to_all(field, 'row', 0, 0, tiled=True)  20.2 us
    all_to_all x5, waiting for transfers between devices, row_exchange(): return lax.all_to_all(field, 'row', 0, 0, tiled=True)  14.2 us
  transfers between devices with their start and end apart: 29, of which 10 were waited for; matrix products, arithmetic and copies ran while one was open for 3% of the time, Pallas kernels for 13%

profile of v2, /device:TPU:0, one launch (start us, length us, event | category | flops | bytes accessed | tf_op | source)
XLA Modules:
  0.0 438.1 jit_solution(1120578086639754985)
XLA Ops:
  5.2 12.5 %head.1 = (f32[8,4,16,8,128]{4,3,2,1,0:T(8,128)}, f32[8,4,16,8,128]{4,3,2,1,0:T(8,128)}, f32[8,4,16,8,128]{4,3,2,1,0:T(8,128)}, f32[16,2,8,256]{3,2,1,0:T(8,128)}) custom-call(s32[18]{0:T(128)} %pad_add_fusion.ints.refs_0_, f32[4]{0:T(128)} %pad_maximum_fusion.2.floats.refs_1_, f32[3,2,16,64,256]{4,3,2,1,0:T(8,128)} %refs_2_.2, ...), custom_call_target="tpu_custom_call" | custom-call | tf_op jit(solution)/shard_map/head/pallas_call | solution.py:431
  17.7 32.0 %all_to_all.35 = f32[8,4,16,8,128]{4,3,2,1,0:T(8,128)} all-to-all(f32[8,4,16,8,128]{4,3,2,1,0:T(8,128)} %get-tuple-element.31), channel_id=1, replica_groups=mesh['row'=8,'col'=4] {'row'}, dimensions={0} | all-to-all | bytes 4194304 | tf_op jit(solution)/shard_map/all_to_all | solution.py:686
  49.7 29.7 %all_to_all.36 = f32[8,4,16,8,128]{4,3,2,1,0:T(8,128)} all-to-all(f32[8,4,16,8,128]{4,3,2,1,0:T(8,128)S(1)} %copy-done.4), channel_id=1, replica_groups=mesh['row'=8,'col'=4] {'row'}, dimensions={0} | all-to-all | bytes 4194304 | tf_op jit(solution)/shard_map/all_to_all | solution.py:686
  95.4 14.1 %all-to-all-done.3 = f32[8,4,16,8,128]{4,3,2,1,0:T(8,128)S(1)} async-done(((f32[8,4,16,8,128]{4,3,2,1,0:T(8,128)}), f32[8,4,16,8,128]{4,3,2,1,0:T(8,128)S(1)}, u32[]{:S(2)}, u32[]{:S(2)}) %all-to-all-start.3) | async-done | bytes 2097184 | tf_op jit(solution)/shard_map/all_to_all | solution.py:686
  115.4 9.7 %collective-permute-start.10 = (f32[88,8,128]{2,1,0:T(8,128)S(1)}, f32[88,8,128]{2,1,0:T(8,128)S(1)}, u32[]{:S(2)}, u32[]{:S(2)}) collective-permute-start(f32[88,8,128]{2,1,0:T(8,128)S(1)} %slice.141), channel_id=1, source_target_pairs={{0,2},{1,3},{2,0},{3,1},{4,6},{5,7},{6,4},{7,5},{8,10},{9,11},{10,... | collective-permute-start | bytes 1081352 | tf_op jit(solution)/shard_map/ppermute | solution.py:681
  134.5 29.3 %collective-permute-done.1.refs_2_ = f32[88,8,128]{2,1,0:T(8,128)S(1)} collective-permute-done((f32[88,8,128]{2,1,0:T(8,128)S(1)}, f32[88,8,128]{2,1,0:T(8,128)S(1)}, u32[]{:S(2)}, u32[]{:S(2)}) %collective-permute-start.1) | collective-permute-done | bytes 360480 | tf_op jit(solution)/shard_map/ppermute | solution.py:681
  172.1 10.2 %shard_map.184 = (f32[88,8,128]{2,1,0:T(8,128)}, f32[88,8,128]{2,1,0:T(8,128)}, f32[88,8,128]{2,1,0:T(8,128)}, f32[88,8,128]{2,1,0:T(8,128)}, f32[88,8,128]{2,1,...) custom-call(s32[18]{0:T(128)} %pad_add_fusion.ints.refs_0_, ...), custom_call_target="tpu_custom_call" | custom-call | tf_op jit(solution)/shard_map/pallas_call | solution.py:570
  183.9 6.8 %to_grid.5.refs_1_.refs_0_ = f32[8,256,256]{2,1,0:T(8,128)} custom-call(s32[18]{0:T(128)} %pad_add_fusion.ints.refs_0_, f32[88,8,128]{2,1,0:T(8,128)} %slice.137.refs_0_, f32[88,8,128]{2,1,0:T(8,128)} %copy-done.15, f32[88,8,128]{2,1,0:T(8,128)} %copy-done.16, f32[88,8,128]{2,1,0:T(8,128)} %copy-done.18, bf16[4,128,512]{2,1,0:T(8,128)(2,1)} %constant.36.clone.refs_4_, ...), custom_call_target="tpu_custom_call" | custom-call | tf_op jit(solution)/shard_map/to_grid/pallas_call | solution.py:482
  190.7 7.6 %shard_map.187 = (f32[88,8,128]{2,1,0:T(8,128)}, f32[88,8,128]{2,1,0:T(8,128)}, f32[88,8,128]{2,1,0:T(8,128)}, f32[88,8,128]{2,1,0:T(8,128)}) custom-call(s32[18]{0:T(128)} %pad_add_fusion.ints.refs_0_, f32[8,256,256]{2,1,0:T(8,128)} %to_grid.5.refs_1_.refs_0_, f32[8,256,256]{2,1,0:T(8,128)} %to_grid.4.refs_1_.refs_2_, ...), custom_call_target="tpu_custom_call" | custom-call | tf_op jit(solution)/shard_map/pallas_call | solution.py:570
  205.2 10.6 %shard_map.185 = (f32[88,8,128]{2,1,0:T(8,128)}, f32[88,8,128]{2,1,0:T(8,128)}, f32[88,8,128]{2,1,0:T(8,128)}, f32[88,8,128]{2,1,0:T(8,128)}, f32[88,8,128]{2,1,...) custom-call(s32[18]{0:T(128)} %pad_add_fusion.ints.refs_0_, ...), custom_call_target="tpu_custom_call" | custom-call | tf_op jit(solution)/shard_map/pallas_call | solution.py:570
  215.8 8.2 %collective-permute-start.12 = (f32[88,8,128]{2,1,0:T(8,128)}, f32[88,8,128]{2,1,0:T(8,128)S(1)}, u32[]{:S(2)}, u32[]{:S(2)}) collective-permute-start(f32[88,8,128]{2,1,0:T(8,128)} %get-tuple-element.39), channel_id=1, source_target_pairs={{0,1},{1,0},{2,3},{3,2},{4,5},{5,4},{6,7},{7,6},{8,9},{9,8},{10,11... | collective-permute-start | bytes 1081352 | tf_op jit(solution)/shard_map/ppermute | solution.py:681
  227.3 13.6 %collective-permute-done.12.refs_1_ = f32[88,8,128]{2,1,0:T(8,128)S(1)} collective-permute-done((f32[88,8,128]{2,1,0:T(8,128)}, f32[88,8,128]{2,1,0:T(8,128)S(1)}, u32[]{:S(2)}, u32[]{:S(2)}) %collective-permute-start.12) | collective-permute-done | bytes 360480 | tf_op jit(solution)/shard_map/ppermute | solution.py:681
  240.9 10.9 %collective-permute-done.14.refs_3_ = f32[88,8,128]{2,1,0:T(8,128)S(1)} collective-permute-done((f32[88,8,128]{2,1,0:T(8,128)}, f32[88,8,128]{2,1,0:T(8,128)S(1)}, u32[]{:S(2)}, u32[]{:S(2)}) %collective-permute-start.14) | collective-permute-done | bytes 360480 | tf_op jit(solution)/shard_map/ppermute | solution.py:681
  261.0 7.2 %collective-permute-start.6 = (f32[88,8,128]{2,1,0:T(8,128)S(1)}, f32[88,8,128]{2,1,0:T(8,128)S(1)}, u32[]{:S(2)}, u32[]{:S(2)}) collective-permute-start(f32[88,8,128]{2,1,0:T(8,128)S(1)} %copy-done.23), channel_id=1, source_target_pairs={{0,1},{1,0},{2,3},{3,2},{4,5},{5,4},{6,7},{7,6},{8,9},{9,8},{10,11... | collective-permute-start | bytes 1081352 | tf_op jit(solution)/shard_map/ppermute | solution.py:681
  271.6 13.3 %collective-permute-done.6.refs_1_ = f32[88,8,128]{2,1,0:T(8,128)S(1)} collective-permute-done((f32[88,8,128]{2,1,0:T(8,128)S(1)}, f32[88,8,128]{2,1,0:T(8,128)S(1)}, u32[]{:S(2)}, u32[]{:S(2)}) %collective-permute-start.6) | collective-permute-done | bytes 360480 | tf_op jit(solution)/shard_map/ppermute | solution.py:681
  284.9 11.0 %collective-permute-done.7.refs_2_ = f32[88,8,128]{2,1,0:T(8,128)S(1)} collective-permute-done((f32[88,8,128]{2,1,0:T(8,128)S(1)}, f32[88,8,128]{2,1,0:T(8,128)S(1)}, u32[]{:S(2)}, u32[]{:S(2)}) %collective-permute-start.7) | collective-permute-done | bytes 360480 | tf_op jit(solution)/shard_map/ppermute | solution.py:681
  305.3 7.4 %collective-permute-start.15 = (f32[88,8,128]{2,1,0:T(8,128)S(1)}, f32[88,8,128]{2,1,0:T(8,128)S(1)}, u32[]{:S(2)}, u32[]{:S(2)}) collective-permute-start(f32[88,8,128]{2,1,0:T(8,128)S(1)} %copy-done.26), channel_id=1, source_target_pairs={{0,1},{1,0},{2,3},{3,2},{4,5},{5,4},{6,7},{7,6},{8,9},{9,8},{10,11... | collective-permute-start | bytes 1081352 | tf_op jit(solution)/shard_map/ppermute | solution.py:681
  316.1 13.1 %collective-permute-done.15.refs_1_ = f32[88,8,128]{2,1,0:T(8,128)S(1)} collective-permute-done((f32[88,8,128]{2,1,0:T(8,128)S(1)}, f32[88,8,128]{2,1,0:T(8,128)S(1)}, u32[]{:S(2)}, u32[]{:S(2)}) %collective-permute-start.15) | collective-permute-done | bytes 360480 | tf_op jit(solution)/shard_map/ppermute | solution.py:681
  329.2 11.2 %collective-permute-done.16.refs_2_ = f32[88,8,128]{2,1,0:T(8,128)S(1)} collective-permute-done((f32[88,8,128]{2,1,0:T(8,128)S(1)}, f32[88,8,128]{2,1,0:T(8,128)S(1)}, u32[]{:S(2)}, u32[]{:S(2)}) %collective-permute-start.16) | collective-permute-done | bytes 360480 | tf_op jit(solution)/shard_map/ppermute | solution.py:681
  350.8 8.9 %collective-permute-start.19 = (f32[8,16,8,128]{3,2,1,0:T(8,128)}, f32[8,16,8,128]{3,2,1,0:T(8,128)}, u32[]{:S(2)}, u32[]{:S(2)}) collective-permute-start(f32[8,16,8,128]{3,2,1,0:T(8,128)} %get-tuple-element.62), channel_id=1, source_target_pairs={{0,2},{1,3},{2,0},{3,1},{4,6},{5,7},{6,4},{7,5},{8,10},{9,11},{10,... | collective-permute-start | bytes 1572872 | tf_op jit(solution)/shard_map/ppermute | solution.py:681
  363.7 31.9 %collective-permute-done.23 = f32[16,2]{1,0:T(8,128)S(1)} collective-permute-done((f32[16,2]{1,0:T(8,128)S(1)}, f32[16,2]{1,0:T(8,128)S(1)}, u32[]{:S(2)}, u32[]{:S(2)}) %collective-permute-start.23) | collective-permute-done | bytes 160 | tf_op jit(solution)/shard_map/ppermute | solution.py:681
  395.7 11.8 %collective-permute-start.21 = (f32[16,2]{1,0:T(8,128)S(1)}, f32[16,2]{1,0:T(8,128)S(1)}, u32[]{:S(2)}, u32[]{:S(2)}) collective-permute-start(f32[16,2]{1,0:T(8,128)S(1)} %reduce_sum.9), channel_id=1, source_target_pairs={{0,1},{1,0},{2,3},{3,2},{4,5},{5,4},{6,7},{7,6},{8,9},{9,8},{10,11... | collective-permute-start | bytes 392 | tf_op jit(solution)/shard_map/ppermute | solution.py:681
  409.9 12.7 %shard_map.186 = (f32[3,2,16,64,256]{4,3,2,1,0:T(8,128)}, f32[3,2,16,64,256]{4,3,2,1,0:T(8,128)}) custom-call(s32[18]{0:T(128)} %pad_add_fusion.ints.refs_0_, f32[4]{0:T(128)} %pad_maximum_fusion.2.floats.refs_1_, f32[3,2,16,64,256]{4,3,2,1,0:T(8,128)} %refs_2_.2, f32[3,2,16,64,256]{4,3,2,1,0:T(8,128)} %refs_3_.3, ...), custom_call_target="tpu_custom_call" | custom-call | tf_op jit(solution)/shard_map/pallas_call | solution.py:664
  426.8 11.2 %shard_map.188 = (f32[3,2,16,64,256]{4,3,2,1,0:T(8,128)}, f32[3,2,16,64,256]{4,3,2,1,0:T(8,128)}) custom-call(s32[18]{0:T(128)} %pad_add_fusion.ints.refs_0_, f32[4]{0:T(128)} %pad_maximum_fusion.2.floats.refs_1_, f32[3,2,16,64,256]{4,3,2,1,0:T(8,128)} %get-tuple-element.42.refs_2_, ...), custom_call_target="tpu_custom_call", output_to_operand_aliasing={{0}: (2, {}), {1}: (3, {})} | custom-call | tf_op jit(solution)/shard_map/pallas_call | solution.py:664
  (127 shorter events, 99.6 us)
Async XLA Ops:
  79.4 30.2 %all-to-all-start.3 = ((f32[8,4,16,8,128]{4,3,2,1,0:T(8,128)}), f32[8,4,16,8,128]{4,3,2,1,0:T(8,128)S(1)}, u32[]{:S(2)}, u32[]{:S(2)}) async-start(f32[8,4,16,8,128]{4,3,2,1,0:T(8,128)} %get-tuple-element.37), calls=%async_computation.3 | async-start | bytes 4194304 | tf_op jit(solution)/shard_map/all_to_all | solution.py:686
  86.6 27.1 %collective-permute-start = (f32[88,8,128]{2,1,0:T(8,128)}, f32[88,8,128]{2,1,0:T(8,128)}, u32[]{:S(2)}, u32[]{:S(2)}) collective-permute-start(f32[88,8,128]{2,1,0:T(8,128)} %slice.123), channel_id=1, source_target_pairs={{0,1},{1,0},{2,3},{3,2},{4,5},{5,4},{6,7},{7,6},{8,9},{9,8},{10,11... | collective-permute-start | bytes 1081352 | tf_op jit(solution)/shard_map/ppermute | solution.py:681
  89.5 25.6 %collective-permute-start.3 = (f32[88,8,128]{2,1,0:T(8,128)}, f32[88,8,128]{2,1,0:T(8,128)}, u32[]{:S(2)}, u32[]{:S(2)}) collective-permute-start(f32[88,8,128]{2,1,0:T(8,128)} %slice.131), channel_id=1, source_target_pairs={{0,1},{1,0},{2,3},{3,2},{4,5},{5,4},{6,7},{7,6},{8,9},{9,8},{10,11... | collective-permute-start | bytes 1081352 | tf_op jit(solution)/shard_map/ppermute | solution.py:681
  89.5 25.9 %collective-permute-start.4 = (f32[88,8,128]{2,1,0:T(8,128)}, f32[88,8,128]{2,1,0:T(8,128)}, u32[]{:S(2)}, u32[]{:S(2)}) collective-permute-start(f32[88,8,128]{2,1,0:T(8,128)} %slice.133), channel_id=1, source_target_pairs={{0,2},{1,3},{2,0},{3,1},{4,6},{5,7},{6,4},{7,5},{8,10},{9,11},{10,... | collective-permute-start | bytes 1081352 | tf_op jit(solution)/shard_map/ppermute | solution.py:681
  93.3 31.8 %collective-permute-start.5 = (f32[88,8,128]{2,1,0:T(8,128)}, f32[88,8,128]{2,1,0:T(8,128)}, u32[]{:S(2)}, u32[]{:S(2)}) collective-permute-start(f32[88,8,128]{2,1,0:T(8,128)} %slice.135), channel_id=1, source_target_pairs={{0,3},{1,2},{2,1},{3,0},{4,7},{5,6},{6,5},{7,4},{8,11},{9,10},{10,... | collective-permute-start | bytes 1081352 | tf_op jit(solution)/shard_map/ppermute | solution.py:681
  110.6 53.3 %collective-permute-start.1 = (f32[88,8,128]{2,1,0:T(8,128)S(1)}, f32[88,8,128]{2,1,0:T(8,128)S(1)}, u32[]{:S(2)}, u32[]{:S(2)}) collective-permute-start(f32[88,8,128]{2,1,0:T(8,128)S(1)} %copy-done.14), channel_id=1, source_target_pairs={{0,2},{1,3},{2,0},{3,1},{4,6},{5,7},{6,4},{7,5},{8,10},{9,11},{10,... | collective-permute-start | bytes 1081352 | tf_op jit(solution)/shard_map/ppermute | solution.py:681
  113.7 50.1 %collective-permute-start.2 = (f32[88,8,128]{2,1,0:T(8,128)S(1)}, f32[88,8,128]{2,1,0:T(8,128)S(1)}, u32[]{:S(2)}, u32[]{:S(2)}) collective-permute-start(f32[88,8,128]{2,1,0:T(8,128)S(1)} %slice.127), channel_id=1, source_target_pairs={{0,3},{1,2},{2,1},{3,0},{4,7},{5,6},{6,5},{7,4},{8,11},{9,10},{10,... | collective-permute-start | bytes 1081352 | tf_op jit(solution)/shard_map/ppermute | solution.py:681
  115.1 67.2 %collective-permute-start.9 = (f32[88,8,128]{2,1,0:T(8,128)S(1)}, f32[88,8,128]{2,1,0:T(8,128)S(1)}, u32[]{:S(2)}, u32[]{:S(2)}) collective-permute-start(f32[88,8,128]{2,1,0:T(8,128)S(1)} %slice.139), channel_id=1, source_target_pairs={{0,1},{1,0},{2,3},{3,2},{4,5},{5,4},{6,7},{7,6},{8,9},{9,8},{10,11... | collective-permute-start | bytes 1081352 | tf_op jit(solution)/shard_map/ppermute | solution.py:681
  115.4 66.9 %collective-permute-start.10 = (f32[88,8,128]{2,1,0:T(8,128)S(1)}, f32[88,8,128]{2,1,0:T(8,128)S(1)}, u32[]{:S(2)}, u32[]{:S(2)}) collective-permute-start(f32[88,8,128]{2,1,0:T(8,128)S(1)} %slice.141), channel_id=1, source_target_pairs={{0,2},{1,3},{2,0},{3,1},{4,6},{5,7},{6,4},{7,5},{8,10},{9,11},{10,... | collective-permute-start | bytes 1081352 | tf_op jit(solution)/shard_map/ppermute | solution.py:681
  125.1 57.2 %collective-permute-start.11 = (f32[88,8,128]{2,1,0:T(8,128)S(1)}, f32[88,8,128]{2,1,0:T(8,128)S(1)}, u32[]{:S(2)}, u32[]{:S(2)}) collective-permute-start(f32[88,8,128]{2,1,0:T(8,128)S(1)} %slice.143), channel_id=1, source_target_pairs={{0,3},{1,2},{2,1},{3,0},{4,7},{5,6},{6,5},{7,4},{8,11},{9,10},{10,... | collective-permute-start | bytes 1081352 | tf_op jit(solution)/shard_map/ppermute | solution.py:681
  201.2 54.2 %all-to-all-start.6 = ((f32[8,4,16,8,128]{4,3,2,1,0:T(8,128)}), f32[8,4,16,8,128]{4,3,2,1,0:T(8,128)S(1)}, u32[]{:S(2)}, u32[]{:S(2)}) async-start(f32[8,4,16,8,128]{4,3,2,1,0:T(8,128)} %spread.7), calls=%async_computation.6 | async-start | bytes 4194304 | tf_op jit(solution)/shard_map/all_to_all | solution.py:686
  225.9 26.0 %collective-permute-start.14 = (f32[88,8,128]{2,1,0:T(8,128)}, f32[88,8,128]{2,1,0:T(8,128)S(1)}, u32[]{:S(2)}, u32[]{:S(2)}) collective-permute-start(f32[88,8,128]{2,1,0:T(8,128)} %get-tuple-element.41), channel_id=1, source_target_pairs={{0,3},{1,2},{2,1},{3,0},{4,7},{5,6},{6,5},{7,4},{8,11},{9,10},{10,... | collective-permute-start | bytes 1081352 | tf_op jit(solution)/shard_map/ppermute | solution.py:681
  256.7 42.8 %all-to-all-start.4 = ((f32[8,4,16,8,128]{4,3,2,1,0:T(8,128)}), f32[8,4,16,8,128]{4,3,2,1,0:T(8,128)S(1)}, u32[]{:S(2)}, u32[]{:S(2)}) async-start(f32[8,4,16,8,128]{4,3,2,1,0:T(8,128)} %spread.5), calls=%async_computation.4 | async-start | bytes 4194304 | tf_op jit(solution)/shard_map/all_to_all | solution.py:686
  268.2 27.7 %collective-permute-start.7 = (f32[88,8,128]{2,1,0:T(8,128)S(1)}, f32[88,8,128]{2,1,0:T(8,128)S(1)}, u32[]{:S(2)}, u32[]{:S(2)}) collective-permute-start(f32[88,8,128]{2,1,0:T(8,128)S(1)} %copy-done.22), channel_id=1, source_target_pairs={{0,2},{1,3},{2,0},{3,1},{4,6},{5,7},{6,4},{7,5},{8,10},{9,11},{10,... | collective-permute-start | bytes 1081352 | tf_op jit(solution)/shard_map/ppermute | solution.py:681
  270.1 25.8 %collective-permute-start.8 = (f32[88,8,128]{2,1,0:T(8,128)S(1)}, f32[88,8,128]{2,1,0:T(8,128)S(1)}, u32[]{:S(2)}, u32[]{:S(2)}) collective-permute-start(f32[88,8,128]{2,1,0:T(8,128)S(1)} %copy-done.21), channel_id=1, source_target_pairs={{0,3},{1,2},{2,1},{3,0},{4,7},{5,6},{6,5},{7,4},{8,11},{9,10},{10,... | collective-permute-start | bytes 1081352 | tf_op jit(solution)/shard_map/ppermute | solution.py:681
  300.9 43.1 %all-to-all-start.2 = ((f32[8,4,16,8,128]{4,3,2,1,0:T(8,128)}), f32[8,4,16,8,128]{4,3,2,1,0:T(8,128)}, u32[]{:S(2)}, u32[]{:S(2)}) async-start(f32[8,4,16,8,128]{4,3,2,1,0:T(8,128)} %spread.4), calls=%async_computation.2 | async-start | bytes 4194304 | tf_op jit(solution)/shard_map/all_to_all | solution.py:686
  312.7 27.7 %collective-permute-start.16 = (f32[88,8,128]{2,1,0:T(8,128)S(1)}, f32[88,8,128]{2,1,0:T(8,128)S(1)}, u32[]{:S(2)}, u32[]{:S(2)}) collective-permute-start(f32[88,8,128]{2,1,0:T(8,128)S(1)} %copy-done.25), channel_id=1, source_target_pairs={{0,2},{1,3},{2,0},{3,1},{4,6},{5,7},{6,4},{7,5},{8,10},{9,11},{10,... | collective-permute-start | bytes 1081352 | tf_op jit(solution)/shard_map/ppermute | solution.py:681
  314.6 25.8 %collective-permute-start.17 = (f32[88,8,128]{2,1,0:T(8,128)S(1)}, f32[88,8,128]{2,1,0:T(8,128)S(1)}, u32[]{:S(2)}, u32[]{:S(2)}) collective-permute-start(f32[88,8,128]{2,1,0:T(8,128)S(1)} %copy-done.24), channel_id=1, source_target_pairs={{0,3},{1,2},{2,1},{3,0},{4,7},{5,6},{6,5},{7,4},{8,11},{9,10},{10,... | collective-permute-start | bytes 1081352 | tf_op jit(solution)/shard_map/ppermute | solution.py:681
  344.1 81.4 %all-to-all-start.5 = ((f32[8,4,16,8,128]{4,3,2,1,0:T(8,128)}), f32[8,4,16,8,128]{4,3,2,1,0:T(8,128)S(1)}, u32[]{:S(2)}, u32[]{:S(2)}) async-start(f32[8,4,16,8,128]{4,3,2,1,0:T(8,128)} %spread.6), calls=%async_computation.5 | async-start | bytes 4194304 | tf_op jit(solution)/shard_map/all_to_all | solution.py:686
  350.8 71.7 %collective-permute-start.19 = (f32[8,16,8,128]{3,2,1,0:T(8,128)}, f32[8,16,8,128]{3,2,1,0:T(8,128)}, u32[]{:S(2)}, u32[]{:S(2)}) collective-permute-start(f32[8,16,8,128]{3,2,1,0:T(8,128)} %get-tuple-element.62), channel_id=1, source_target_pairs={{0,2},{1,3},{2,0},{3,1},{4,6},{5,7},{6,4},{7,5},{8,10},{9,11},{10,... | collective-permute-start | bytes 1572872 | tf_op jit(solution)/shard_map/ppermute | solution.py:681
  359.7 62.8 %collective-permute-start.18 = (f32[8,16,8,128]{3,2,1,0:T(8,128)}, f32[8,16,8,128]{3,2,1,0:T(8,128)}, u32[]{:S(2)}, u32[]{:S(2)}) collective-permute-start(f32[8,16,8,128]{3,2,1,0:T(8,128)} %get-tuple-element.63), channel_id=1, source_target_pairs={{0,1},{1,0},{2,3},{3,2},{4,5},{5,4},{6,7},{7,6},{8,9},{9,8},{10,11... | collective-permute-start | bytes 1572872 | tf_op jit(solution)/shard_map/ppermute | solution.py:681
  359.7 62.8 %collective-permute-start.20 = (f32[8,16,8,128]{3,2,1,0:T(8,128)S(1)}, f32[8,16,8,128]{3,2,1,0:T(8,128)}, u32[]{:S(2)}, u32[]{:S(2)}) collective-permute-start(f32[8,16,8,128]{3,2,1,0:T(8,128)S(1)} %get-tuple-element.64), channel_id=1, source_target_pairs={{0,3},{1,2},{2,1},{3,0},{4,7},{5,6},{6,5},{7,4},{8,11},{9,10},{10,... | collective-permute-start | bytes 1572872 | tf_op jit(solution)/shard_map/ppermute | solution.py:681
  361.3 34.4 %collective-permute-start.23 = (f32[16,2]{1,0:T(8,128)S(1)}, f32[16,2]{1,0:T(8,128)S(1)}, u32[]{:S(2)}, u32[]{:S(2)}) collective-permute-start(f32[16,2]{1,0:T(8,128)S(1)} %reduce_sum.9), channel_id=1, source_target_pairs={{0,3},{1,2},{2,1},{3,0},{4,7},{5,6},{6,5},{7,4},{8,11},{9,10},{10,... | collective-permute-start | bytes 392 | tf_op jit(solution)/shard_map/ppermute | solution.py:681
  363.7 43.7 %collective-permute-start.22 = (f32[16,2]{1,0:T(8,128)S(1)}, f32[16,2]{1,0:T(8,128)S(1)}, u32[]{:S(2)}, u32[]{:S(2)}) collective-permute-start(f32[16,2]{1,0:T(8,128)S(1)} %reduce_sum.9), channel_id=1, source_target_pairs={{0,2},{1,3},{2,0},{3,1},{4,6},{5,7},{6,4},{7,5},{8,10},{9,11},{10,... | collective-permute-start | bytes 392 | tf_op jit(solution)/shard_map/ppermute | solution.py:681
  (32 other events, 275.4 us)
